TPU v7x, 32 devices: a whole 2x2x4 slice. The times are simulated.
32 devices in a mesh: cp: 8 (over z, x), tp: 4 (over y, core).
Axes of the slice: x: 2, y: 2, z: 4, core: 2. Of those that a mesh axis runs over, the one named last changes fastest.
Arguments:
- queries: bfloat16 [1024, 8192], P('cp', 'tp'), may hold values from -6 to 6
- keys: bfloat16 [1024, 1024], P('cp', 'tp'), may hold values from -6 to 6
- values: bfloat16 [1024, 1024], P('cp', 'tp'), may hold values from -6 to 6
- doc_blocks: int32 [4], replicated, may hold values from 1 to 4, 8 in all
- block_order: int32 [8], replicated, may hold values from 0 to 7, each once
- out_weight: bfloat16 [8192, 4096], P('tp'), may hold values from -0.5 to 0.5
Outputs:
- layer_out: bfloat16 [1024, 4096], P(('cp', 'tp'))
Inputs may be any that keep to these rules, and one draw needn't show every extreme that they name: Array block i (rows i * 128 to i * 128 + 127) holds sequence block block_order[i]; every block number appears once. `doc_blocks`: they sum to 8; the longest document has exactly 4 blocks.
All inputs are finite; a program needn't handle non-finite values.
Results may differ from a plain program's by a relative error of at most 0.013.
Values may be sent and summed in bfloat16 or wider, within the bound.
No kernel may reach another device: no remote copies, remote signals or barrier semaphores. Data moves between devices by JAX's collectives and lax.ppermute only.
A program may use at most 128 MiB of HBM per device.

v0:
```python
import jax
import jax.numpy as jnp
from jax import lax
from jax.sharding import PartitionSpec as P

HEAD_SIZE = 128
BLOCK_TOKENS = 128


document_masked_score = -1e30


def lookup(entries, indices):
    matches = indices[:, None] == jnp.arange(entries.shape[0], dtype=jnp.int32)[None, :]
    return jnp.sum(jnp.where(matches, entries[None, :], 0), axis=1)


def locate(row_ids, block_order, doc_ends):
    seq_block = lookup(block_order, row_ids // BLOCK_TOKENS)
    position = seq_block * BLOCK_TOKENS + row_ids % BLOCK_TOKENS
    doc_ids = jnp.sum((seq_block[:, None] >= doc_ends[None, :]).astype(jnp.int32), axis=1)
    return (position, doc_ids)


def attend(online, key_rows, value_rows, key_pos, key_doc, query_rows, query_pos, query_doc):
    allowed = (query_doc[:, None] == key_doc[None, :]) & (key_pos[None, :] <= query_pos[:, None])
    running_max, weight_sum, weighted = online
    scores = jnp.einsum(
        "qhgd,khd->hgqk", query_rows, key_rows, preferred_element_type=jnp.float32
    ) * HEAD_SIZE ** (-0.5)
    scores = jnp.where(allowed, scores, document_masked_score)
    new_max = jnp.maximum(running_max, jnp.max(scores, axis=-1))
    weights = jnp.where(allowed, jnp.exp(scores - new_max[..., None]), 0.0)
    factor = jnp.exp(running_max - new_max)
    weight_sum = weight_sum * factor + jnp.sum(weights, axis=-1)
    weighted = weighted * factor[..., None] + jnp.einsum(
        "hgqk,khd->hgqd",
        weights.astype(jnp.bfloat16),
        value_rows,
        preferred_element_type=jnp.float32,
    )
    return (new_max, weight_sum, weighted)


def sweep_keys(
    online, key_part, value_part, block_order, doc_ends, query_rows, query_pos, query_doc
):
    length = key_part.shape[0]
    heads_kv = key_part.shape[1] // HEAD_SIZE
    block_rows = 512
    token_blocks = length // block_rows
    key_pos, key_doc = locate(jnp.arange(length, dtype=jnp.int32), block_order, doc_ends)

    def scan_step(status, pieces_now):
        return (
            attend(
                status,
                pieces_now[0],
                pieces_now[1],
                pieces_now[2],
                pieces_now[3],
                query_rows,
                query_pos,
                query_doc,
            ),
            None,
        )

    online, unused = lax.scan(
        scan_step,
        online,
        (
            key_part.reshape(token_blocks, block_rows, heads_kv, HEAD_SIZE),
            value_part.reshape(token_blocks, block_rows, heads_kv, HEAD_SIZE),
            key_pos.reshape(token_blocks, block_rows),
            key_doc.reshape(token_blocks, block_rows),
        ),
    )
    return online


def local(queries, keys, values, doc_blocks, block_order, out_weight):
    rows_dev = queries.shape[0]
    heads_kv = keys.shape[1] // HEAD_SIZE
    group_size = queries.shape[1] // keys.shape[1]
    doc_ends = jnp.cumsum(doc_blocks)
    first_row = lax.axis_index("cp") * rows_dev
    query_pos, query_doc = locate(
        first_row + jnp.arange(rows_dev, dtype=jnp.int32), block_order, doc_ends
    )
    query_rows = queries.reshape(rows_dev, heads_kv, group_size, HEAD_SIZE)
    starting_state = (
        jnp.full((heads_kv, group_size, rows_dev), document_masked_score, jnp.float32),
        jnp.zeros((heads_kv, group_size, rows_dev), jnp.float32),
        jnp.zeros((heads_kv, group_size, rows_dev, HEAD_SIZE), jnp.float32),
    )
    whole_keys, whole_values = (
        lax.all_gather(keys, "cp", axis=0, tiled=True),
        lax.all_gather(values, "cp", axis=0, tiled=True),
    )
    running_max, weight_sum, weighted = sweep_keys(
        starting_state,
        whole_keys,
        whole_values,
        block_order,
        doc_ends,
        query_rows,
        query_pos,
        query_doc,
    )
    attended = (
        jnp.transpose(weighted / weight_sum[..., None], (2, 0, 1, 3))
        .reshape(rows_dev, -1)
        .astype(jnp.bfloat16)
    )
    summed = lax.psum_scatter(
        jnp.dot(attended, out_weight, preferred_element_type=jnp.float32).astype(jnp.bfloat16),
        "tp",
        scatter_dimension=0,
        tiled=True,
    )
    return summed


def solution(mesh):
    placed = (P("cp", "tp"), P("cp", "tp"), P("cp", "tp"), P(), P(), P("tp", None))
    return jax.shard_map(
        local, mesh=mesh, in_specs=placed, out_specs=P(("cp", "tp"), None), check_vma=False
    )
```

profile of v0, /device:TPU:0, one launch (start us, length us, event | category | flops | bytes accessed | tf_op | source)
XLA Modules:
  0.0 126.7 jit_solution(15439644955548890981)
XLA Ops:
  6.5 0.0 reduce-scatter.2.cloned.1.call-start
  6.5 0.8 reduce-window.8
  7.4 0.7 select_reduce_fusion.1
  8.1 0.1 convert_reduce_fusion.1
  8.2 0.7 select_reduce_fusion
  9.0 0.1 convert_reduce_fusion
  9.1 1.3 %copy.15 = bf16[128,2048]{0,1:T(8,128)(2,1)S(1)} copy(bf16[128,2048]{1,0:T(8,128)(2,1)} %param.8) | data formatting | bytes 1048576 | tf_op args[0]
  10.4 0.3 copy.17
  10.7 33.3 %all_gather.6 = bf16[1024,256]{1,0:T(8,128)(2,1)S(1)} all-gather(bf16[128,256]{1,0:T(8,128)(2,1)} %param.9), channel_id=1, replica_groups=mesh['cp'=8,'tp'=4] {'cp'}, dimensions={0}, use_global_device_ids=true | all-gather | bytes 589824 | tf_op jit(solution)/shard_map/all_gather | solution.py:98
  44.0 0.1 reshape.86
  44.1 31.5 %all_gather.7 = bf16[1024,256]{1,0:T(8,128)(2,1)S(1)} all-gather(bf16[128,256]{1,0:T(8,128)(2,1)} %param.10), channel_id=1, replica_groups=mesh['cp'=8,'tp'=4] {'cp'}, dimensions={0}, use_global_device_ids=true | all-gather | bytes 589824 | tf_op jit(solution)/shard_map/all_gather | solution.py:99
  75.6 0.1 reshape.88
  75.7 8.3 %while.15 = (s32[]{:T(128)}, f32[2,8,128]{2,1,0:T(8,128)S(1)}, f32[2,8,128]{2,1,0:T(8,128)S(1)}, f32[2,8,128,128]{3,2,1,0:T(8,128)S(1)}, s32[128]{0:T(128)S(1)},...) while((s32[]{:T(128)}, f32[2,8,128]{2,1,0:T(8,128)S(1)}, ...), condition=%wide.region_8.9_spmd.clone, body=%wide.region_5.8_spmd.clone.sunk | while | flops 551495680 | bytes 17183896 | solution.py:69
  75.8 0.2 compare_and_fusion.2
  76.0 0.4 constant_dynamic-slice_fusion.7
  76.4 0.8 fusion.31
  77.2 1.0 fusion.32
  78.2 1.7 %fusion.34 = f32[2,8,128,128]{3,2,1,0:T(8,128)S(1)} fusion(f32[2,512,128,8]{2,1,3,0:T(8,128)S(1)} %get-tuple-element.232, f32[2,8,128]{2,1,0:T(8,128)S(1)} %select_maximum_fusion.2, pred[128,512]{0,1:T(8,128)(4,1)S(1)} %compare_and_fusion.2, f32[2,8,128,128]{3,2,1,0:T(8,128)S(1)} %get-tuple-element.252, f32[2,8,128]{2,1,0:T(8,128)S(1)} %get-tuple-element.234, ...), kind=kOutput, calls=%fused_computation.7.clone.1 | convolution fusion | flops 274464768 | bytes 6635521 | tf_op jit(solution)/shard_map/while/body/eval_jaxpr/hgqk,khd->hgqd/dot_general | solution.py:36
  80.0 0.2 compare_and_fusion.2
  80.2 0.4 constant_dynamic-slice_fusion.7
  80.5 0.8 fusion.31
  81.3 1.0 fusion.32
  82.4 1.7 %fusion.34 = f32[2,8,128,128]{3,2,1,0:T(8,128)S(1)} fusion(f32[2,512,128,8]{2,1,3,0:T(8,128)S(1)} %get-tuple-element.232, f32[2,8,128]{2,1,0:T(8,128)S(1)} %select_maximum_fusion.2, pred[128,512]{0,1:T(8,128)(4,1)S(1)} %compare_and_fusion.2, f32[2,8,128,128]{3,2,1,0:T(8,128)S(1)} %get-tuple-element.252, f32[2,8,128]{2,1,0:T(8,128)S(1)} %get-tuple-element.234, ...), kind=kOutput, calls=%fused_computation.7.clone.1 | convolution fusion | flops 274464768 | bytes 6635521 | tf_op jit(solution)/shard_map/while/body/eval_jaxpr/hgqk,khd->hgqd/dot_general | solution.py:36
  84.1 0.3 copy.19
  84.4 0.1 divide_convert_fusion
  84.6 9.1 %convolution_convert_fusion = bf16[128,4096]{1,0:T(8,128)(2,1)} fusion(bf16[128,2048]{0,1:T(8,128)(2,1)S(1)} %bitcast.54, bf16[2048,4096]{1,0:T(8,128)(2,1)} %param.13), kind=kOutput, calls=%fused_computation.24 | convolution fusion | flops 2148007936 | bytes 18350080 | tf_op jit(solution)/shard_map/dot_general | solution.py:117
  93.7 0.0 reduce-scatter.2.cloned.1.call-update
  93.7 26.1 %reduce-scatter.2.cloned.1.call-done = bf16[32,4096]{1,0:T(8,128)(2,1)} async-done(((bf16[128,4096]{1,0:T(8,128)(2,1)}), bf16[32,4096]{1,0:T(8,128)(2,1)}) %reduce-scatter.2.cloned.1.call-update) | async-done | bytes 262160 | tf_op jit(solution)/shard_map/reduce_scatter | solution.py:116
  (18 shorter events, 0.1 us)
Async XLA Ops:
  6.5 113.3 %reduce-scatter.2.cloned.1.call-start = ((), (), s32[]{:S(2)}) async-start(), calls=%async_computation.1 | async-start | bytes 1310720 | tf_op jit(solution)/shard_map/reduce_scatter | solution.py:116
Sparse Core Ops, SparseCore 0:
  93.9 25.9 reduce-scatter.1
where the time goes:
time: 127 us
  blocking collectives  64.8 us (51%)
  waiting for transfers between devices  26.2 us (21%)
  matrix products  14.1 us (11%)
  between operations  13.5 us (11%)
  other arithmetic  5.09 us (4%)
  local copies, waits for them, and re-layouts  2.96 us (2%)
    all_gather x1, blocking collectives, local(): lax.all_gather(keys, 'cp', axis=0, tiled=True)  33.3 us
    all_gather x1, blocking collectives, local(): lax.all_gather(values, 'cp', axis=0, tiled=True)  31.5 us
    reduce_scatter x1, waiting for transfers between devices, local(): lax.psum_scatter(jnp.dot(attended, out_weight, preferred_element_type=jnp...  26.1 us
    dot_general x1, matrix products, local(): jnp.dot(attended, out_weight, preferred_element_type=jnp.float32)  9.15 us
    dot_general x2, matrix products, attend(): jnp.einsum('hgqk,khd->hgqd', weights.astype(jnp.bfloat16), value_rows, pr...  3.43 us
  transfers between devices with their start and end apart: 1, of which 1 were waited for; matrix products, arithmetic and copies ran while one was open for 0% of the time, Pallas kernels for 0%

commit v1 on v0

--- a/solution.py
+++ b/solution.py
@@ -1,13 +1,15 @@
+import functools
+
 import jax
 import jax.numpy as jnp
 from jax import lax
+from jax.experimental import pallas as pl
+from jax.experimental.pallas import tpu as pltpu
 from jax.sharding import PartitionSpec as P
 
 HEAD_SIZE = 128
 BLOCK_TOKENS = 128
-
-
-document_masked_score = -1e30
+MASKED = -1e30
 
 
 def lookup(entries, indices):
@@ -28,7 +30,7 @@
     scores = jnp.einsum(
         "qhgd,khd->hgqk", query_rows, key_rows, preferred_element_type=jnp.float32
     ) * HEAD_SIZE ** (-0.5)
-    scores = jnp.where(allowed, scores, document_masked_score)
+    scores = jnp.where(allowed, scores, MASKED)
     new_max = jnp.maximum(running_max, jnp.max(scores, axis=-1))
     weights = jnp.where(allowed, jnp.exp(scores - new_max[..., None]), 0.0)
     factor = jnp.exp(running_max - new_max)
@@ -47,24 +49,12 @@
 ):
     length = key_part.shape[0]
     heads_kv = key_part.shape[1] // HEAD_SIZE
-    block_rows = 512
+    block_rows = 4 * BLOCK_TOKENS
     token_blocks = length // block_rows
     key_pos, key_doc = locate(jnp.arange(length, dtype=jnp.int32), block_order, doc_ends)
 
     def scan_step(status, pieces_now):
-        return (
-            attend(
-                status,
-                pieces_now[0],
-                pieces_now[1],
-                pieces_now[2],
-                pieces_now[3],
-                query_rows,
-                query_pos,
-                query_doc,
-            ),
-            None,
-        )
+        return attend(status, *pieces_now, query_rows, query_pos, query_doc), None
 
     online, unused = lax.scan(
         scan_step,
@@ -79,7 +69,7 @@
     return online
 
 
-def local(queries, keys, values, doc_blocks, block_order, out_weight):
+def general(queries, keys, values, doc_blocks, block_order, out_weight):
     rows_dev = queries.shape[0]
     heads_kv = keys.shape[1] // HEAD_SIZE
     group_size = queries.shape[1] // keys.shape[1]
@@ -90,39 +80,174 @@
     )
     query_rows = queries.reshape(rows_dev, heads_kv, group_size, HEAD_SIZE)
     starting_state = (
-        jnp.full((heads_kv, group_size, rows_dev), document_masked_score, jnp.float32),
+        jnp.full((heads_kv, group_size, rows_dev), MASKED, jnp.float32),
         jnp.zeros((heads_kv, group_size, rows_dev), jnp.float32),
         jnp.zeros((heads_kv, group_size, rows_dev, HEAD_SIZE), jnp.float32),
     )
-    whole_keys, whole_values = (
-        lax.all_gather(keys, "cp", axis=0, tiled=True),
-        lax.all_gather(values, "cp", axis=0, tiled=True),
-    )
+    whole_keys = lax.all_gather(keys, "cp", axis=0, tiled=True)
+    whole_values = lax.all_gather(values, "cp", axis=0, tiled=True)
     running_max, weight_sum, weighted = sweep_keys(
-        starting_state,
-        whole_keys,
-        whole_values,
-        block_order,
-        doc_ends,
-        query_rows,
-        query_pos,
-        query_doc,
+        starting_state, whole_keys, whole_values, block_order, doc_ends,
+        query_rows, query_pos, query_doc,
     )
     attended = (
         jnp.transpose(weighted / weight_sum[..., None], (2, 0, 1, 3))
         .reshape(rows_dev, -1)
         .astype(jnp.bfloat16)
     )
-    summed = lax.psum_scatter(
+    return lax.psum_scatter(
         jnp.dot(attended, out_weight, preferred_element_type=jnp.float32).astype(jnp.bfloat16),
         "tp",
         scatter_dimension=0,
         tiled=True,
     )
-    return summed
+
+
+def attend_project(n_blocks, n_tp, order_ref, docs_ref, q_ref, *refs):
+    kv_refs, (w_hbm, give_ref, keep_ref, w_ref, kv_ref, att_ref, bias_ref, seq_ref, sems) = (
+        refs[:n_blocks], refs[n_blocks:])
+    n_docs = docs_ref.shape[0]
+    n_slots = kv_ref.shape[0]
+    n_chunks, _, chunk = w_ref.shape
+    rows, width = q_ref.shape
+    part = rows // n_tp
+    heads_kv = kv_refs[0].shape[1] // HEAD_SIZE
+    group = width // HEAD_SIZE // heads_kv
+    me, core = lax.axis_index("cp"), lax.axis_index("tp")
+
+    loads = [
+        pltpu.make_async_copy(w_hbm.at[:, pl.ds(j * chunk, chunk)], w_ref.at[j], sems.at[j])
+        for j in range(n_chunks)
+    ]
+    for load in loads:
+        load.start()
+
+    ends = []
+    for d in range(n_docs):
+        ends.append(docs_ref[d] + (ends[-1] if ends else 0))
+
+    def document(seq):
+        return sum((seq >= end).astype(jnp.int32) for end in ends)
+
+    own_seq = order_ref[me]
+    own_doc = document(own_seq)
+    for slot in range(n_slots):
+        kv_ref[slot] = kv_refs[0][...]
+        seq_ref[slot] = own_seq if slot == 0 else own_seq + 1
+    used = jnp.int32(1)
+    for s in range(1, n_blocks):
+        seq = order_ref[me ^ s]
+        wanted = (document(seq) == own_doc) & (seq < own_seq)
+
+        @pl.when(wanted)
+        def _(s=s, seq=seq, used=used):
+            kv_ref[used] = kv_refs[s][...]
+            seq_ref[used] = seq
+
+        used = used + wanted.astype(jnp.int32)
+
+    targets = [core ^ f for f in (3, 1, 2, 0)]
+    key_at = lax.broadcasted_iota(jnp.int32, (part, BLOCK_TOKENS), 1)
+    row_at = lax.broadcasted_iota(jnp.int32, (part, BLOCK_TOKENS), 0)
+    for slot in range(n_slots):
+        ahead = (own_seq - seq_ref[slot]) * BLOCK_TOKENS
+        for p, target in enumerate(targets):
+            bias_ref[p * part : (p + 1) * part, slot * BLOCK_TOKENS : (slot + 1) * BLOCK_TOKENS] = (
+                jnp.where(key_at <= row_at + (target * part + ahead), 0.0, MASKED)
+            )
+
+    def query(h):
+        return [
+            q_ref[pl.ds(pl.multiple_of(t * part, part), part), h * HEAD_SIZE : (h + 1) * HEAD_SIZE]
+            for t in targets
+        ]
+
+    scale = HEAD_SIZE**-0.5 * 1.4426950408889634
+    ones = jnp.ones((n_slots * BLOCK_TOKENS, HEAD_SIZE), jnp.bfloat16)
+    for g in range(heads_kv):
+        cols = slice(g * HEAD_SIZE, (g + 1) * HEAD_SIZE)
+        key_rows = jnp.concatenate([kv_ref[j, :BLOCK_TOKENS, cols] for j in range(n_slots)], 0)
+        value_rows = jnp.concatenate([kv_ref[j, BLOCK_TOKENS:, cols] for j in range(n_slots)], 0)
+        value_rows = jnp.concatenate([value_rows, ones], 1)
+        for h in range(g * group, (g + 1) * group):
+            scores = lax.dot_general(
+                jnp.concatenate(query(h), 0), key_rows, (((1,), (1,)), ((), ())),
+                preferred_element_type=jnp.float32,
+            ) + bias_ref[...]
+            top = jnp.max(scores, axis=1, keepdims=True)
+            weights = jnp.exp2((scores - top) * scale).astype(jnp.bfloat16)
+            sums = jnp.dot(weights, value_rows, preferred_element_type=jnp.float32)
+            att_ref[:, h * HEAD_SIZE : (h + 1) * HEAD_SIZE] = (
+                sums[:, :HEAD_SIZE] / sums[:, HEAD_SIZE:]
+            ).astype(jnp.bfloat16)
+
+    half = rows // 2
+    for j, load in enumerate(loads):
+        load.wait()
+        product = jnp.dot(att_ref[...], w_ref[j], preferred_element_type=jnp.float32)
+        give_ref[:, j * chunk : (j + 1) * chunk] = product[:half].astype(jnp.bfloat16)
+        keep_ref[:, j * chunk : (j + 1) * chunk] = product[half:]
+
+
+def exchange(kv, n):
+    def swap(block, s):
+        return lax.ppermute(block, "cp", [(i, i ^ s) for i in range(n)])
+
+    got = {0: kv}
+    for s in range(2, n, 2):
+        got[s] = swap(kv, s)
+    for s in range(0, n, 2):
+        got[s + 1] = swap(got[s], 1)
+    return [got[s] for s in range(n)]
+
+
+def blockwise(n, n_tp, queries, keys, values, doc_blocks, block_order, out_weight):
+    rows, width = queries.shape
+    out_width = out_weight.shape[1]
+    blocks = exchange(jnp.concatenate([keys, values], 0), n)
+    n_slots = n // 2
+    chunk = out_width // 8
+    smem = pl.BlockSpec(memory_space=pltpu.SMEM)
+    vmem = pl.BlockSpec(memory_space=pltpu.VMEM)
+    give, keep = pl.pallas_call(
+        functools.partial(attend_project, n, n_tp),
+        out_shape=(
+            jax.ShapeDtypeStruct((rows // 2, out_width), jnp.bfloat16),
+            jax.ShapeDtypeStruct((rows // 2, out_width), jnp.float32),
+        ),
+        in_specs=[smem, smem] + [vmem] * (n + 1) + [pl.BlockSpec(memory_space=pltpu.HBM)],
+        out_specs=(vmem, vmem),
+        scratch_shapes=[
+            pltpu.VMEM((8, width, chunk), jnp.bfloat16),
+            pltpu.VMEM((n_slots,) + blocks[0].shape, jnp.bfloat16),
+            pltpu.VMEM((rows, width), jnp.bfloat16),
+            pltpu.VMEM((rows, n_slots * BLOCK_TOKENS), jnp.float32),
+            pltpu.SMEM((n_slots,), jnp.int32),
+            pltpu.SemaphoreType.DMA((8,)),
+        ],
+        compiler_params=pltpu.CompilerParams(vmem_limit_bytes=40 * 1024 * 1024),
+        cost_estimate=pl.CostEstimate(
+            flops=2 * rows * width * out_width, bytes_accessed=2 * width * out_width,
+            transcendentals=0),
+        name="attend_project",
+    )(block_order, doc_blocks, queries, *blocks, out_weight)
+    part = rows // n_tp
+    got = lax.ppermute(give, "tp", [(i, i ^ 1) for i in range(n_tp)])
+    far = (keep[:part] + got[:part].astype(jnp.float32)).astype(jnp.bfloat16)
+    near = keep[part:] + got[part:].astype(jnp.float32)
+    crossed = lax.ppermute(far, "tp", [(i, i ^ 2) for i in range(n_tp)])
+    return (near + crossed.astype(jnp.float32)).astype(jnp.bfloat16)
 
 
 def solution(mesh):
+    n, n_tp = mesh.shape["cp"], mesh.shape["tp"]
+
+    def local(queries, keys, values, doc_blocks, block_order, out_weight):
+        args = (queries, keys, values, doc_blocks, block_order, out_weight)
+        if n == 8 and n_tp == 4 and queries.shape[0] == BLOCK_TOKENS:
+            return blockwise(n, n_tp, *args)
+        return general(*args)
+
     placed = (P("cp", "tp"), P("cp", "tp"), P("cp", "tp"), P(), P(), P("tp", None))
     return jax.shard_map(
         local, mesh=mesh, in_specs=placed, out_specs=P(("cp", "tp"), None), check_vma=False

time: 127 us -> 46.1 us (0.36)
  blocking collectives: 64.8 us -> 0 us
  matrix products: 14.1 us -> 0 us
  between operations: 13.5 us -> 0.03 us
  starting transfers between devices: 0.01 us -> 12.7 us
  Pallas kernels: 0 us -> 7.03 us
  waiting for transfers between devices: 26.2 us -> 21.2 us
  other arithmetic: 5.09 us -> 0.87 us
    all_gather x2 -> x0, blocking collectives: 64.8 us -> none  [the longest x1 33.3 us: local(): lax.all_gather(keys, 'cp', axis=0, tiled=True)]
    reduce_scatter x1 -> x0, waiting for transfers between devices: 26.1 us -> none  [local(): lax.psum_scatter(jnp.dot(attended, out_weight, preferred_element_type=jnp...]
    ppermute x0 -> x9, waiting for transfers between devices: none -> 21.2 us  [the longest x7 12.5 us: swap(): return lax.ppermute(block, 'cp', [(i, i ^ s) for i in range(n)])]
    dot_general x5 -> x0, matrix products: 14.1 us -> none  [the longest x1 9.15 us: local(): jnp.dot(attended, out_weight, preferred_element_type=jnp.float32)]
    ppermute x0 -> x9, starting transfers between devices: none -> 12.7 us  [the longest x7 11 us: swap(): return lax.ppermute(block, 'cp', [(i, i ^ s) for i in range(n)])]
    pallas_call x0 -> x1, Pallas kernels: none -> 7.03 us  [blockwise(): pl.pallas_call(functools.partial(attend_project, n, n_tp), out_shape=(jax...]
    reduce_sum x6 -> x0, other arithmetic: 3.65 us -> none  [the longest x2 2.01 us: attend(): weight_sum = weight_sum * factor + jnp.sum(weights, axis=-1)]
    unnamed x2 -> x7, local copies, waits for them, and re-layouts: 1.6 us -> 3.19 us
  transfers between devices with their start and end apart: 1 -> 9, of which waited for: 1 -> 6; matrix products, arithmetic and copies ran while one was open for 0% -> 0% of each run, Pallas kernels for 0% -> 0%
where the time goes in v1:
time: 46.1 us; the launch traced here: 45.9 us
  waiting for transfers between devices  21.2 us (46%)
  starting transfers between devices  12.7 us (28%)
  Pallas kernels  7.03 us (15%)
  local copies, waits for them, and re-layouts  4.04 us (9%)
  other arithmetic  0.87 us (2%)
    ppermute x7, waiting for transfers between devices, swap(): return lax.ppermute(block, 'cp', [(i, i ^ s) for i in range(n)])  12.5 us
    ppermute x7, starting transfers between devices, swap(): return lax.ppermute(block, 'cp', [(i, i ^ s) for i in range(n)])  11 us
    pallas_call x1, Pallas kernels, blockwise(): pl.pallas_call(functools.partial(attend_project, n, n_tp), out_shape=(jax...  7.03 us
    ppermute x1, waiting for transfers between devices, blockwise(): crossed = lax.ppermute(far, 'tp', [(i, i ^ 2) for i in range(n_tp)])  6.83 us
    unnamed x7, local copies, waits for them, and re-layouts  3.19 us
    ppermute x1, waiting for transfers between devices, blockwise(): got = lax.ppermute(give, 'tp', [(i, i ^ 1) for i in range(n_tp)])  1.9 us
    ppermute x1, starting transfers between devices, blockwise(): crossed = lax.ppermute(far, 'tp', [(i, i ^ 2) for i in range(n_tp)])  1.58 us
  transfers between devices with their start and end apart: 9, of which 6 were waited for; matrix products, arithmetic and copies ran while one was open for 0% of the time, Pallas kernels for 0%

profile of v1, /device:TPU:0, one launch (start us, length us, event | category | flops | bytes accessed | tf_op | source)
XLA Modules:
  0.0 45.9 jit_solution(12592407426640093473)
XLA Ops:
  0.0 0.8 %constant_dynamic-update-slice_fusion.1 = bf16[256,256]{1,0:T(8,128)(2,1)S(1)} fusion(bf16[128,256]{1,0:T(8,128)(2,1)} %param.7), kind=kLoop, calls=%fused_computation.3 | loop fusion | bytes 131072
  0.8 0.8 %constant_dynamic-update-slice_fusion.refs_0_ = bf16[256,256]{1,0:T(8,128)(2,1)S(1)} fusion(bf16[256,256]{1,0:T(8,128)(2,1)S(1)} %constant_dynamic-update-slice_fusion.1, bf16[128,256]{1,0:T(8,128)(2,1)} %param.8), kind=kLoop, calls=%fused_computation.2 | loop fusion | bytes 131072 | tf_op jit(solution)/shard_map/concatenate | solution.py:207
  1.7 5.1 %collective-permute-start.5 = (bf16[256,256]{1,0:T(8,128)(2,1)S(1)}, bf16[256,256]{1,0:T(8,128)(2,1)S(1)}, u32[]{:S(2)}, u32[]{:S(2)}) collective-permute-start(bf16[256,256]{1,0:T(8,128)(2,1)S(1)} %constant_dynamic-update-slice_fusion.refs_0_), channel_id=1, source_target_pairs={{0,24},{4,28},{8,16},{12,20},{16,8},{20,12},{24,0},{28,4},{1,25},{... | collective-permute-start | bytes 393224 | tf_op jit(solution)/shard_map/ppermute | solution.py:194
  6.8 0.0 collective-permute-start.3
  6.8 0.6 %collective-permute-start.1 = (bf16[256,256]{1,0:T(8,128)(2,1)S(1)}, bf16[256,256]{1,0:T(8,128)(2,1)S(1)}, u32[]{:S(2)}, u32[]{:S(2)}) collective-permute-start(bf16[256,256]{1,0:T(8,128)(2,1)S(1)} %constant_dynamic-update-slice_fusion.refs_0_), channel_id=1, source_target_pairs={{0,8},{4,12},{8,0},{12,4},{16,24},{20,28},{24,16},{28,20},{1,9},{5... | collective-permute-start | bytes 393224 | tf_op jit(solution)/shard_map/ppermute | solution.py:194
  7.3 1.7 %collective-permute-start = (bf16[256,256]{1,0:T(8,128)(2,1)S(1)}, bf16[256,256]{1,0:T(8,128)(2,1)S(1)}, u32[]{:S(2)}, u32[]{:S(2)}) collective-permute-start(bf16[256,256]{1,0:T(8,128)(2,1)S(1)} %constant_dynamic-update-slice_fusion.refs_0_), channel_id=1, source_target_pairs={{0,4},{4,0},{8,12},{12,8},{16,20},{20,16},{24,28},{28,24},{1,5},{5... | collective-permute-start | bytes 393224 | tf_op jit(solution)/shard_map/ppermute | solution.py:194
  9.0 2.2 %collective-permute-done.5.refs_6_ = bf16[256,256]{1,0:T(8,128)(2,1)S(1)} collective-permute-done((bf16[256,256]{1,0:T(8,128)(2,1)S(1)}, bf16[256,256]{1,0:T(8,128)(2,1)S(1)}, u32[]{:S(2)}, u32[]{:S(2)}) %collective-permute-start.5) | collective-permute-done | bytes 131104 | tf_op jit(solution)/shard_map/ppermute | solution.py:194
  11.2 1.7 %collective-permute-start.6 = (bf16[256,256]{1,0:T(8,128)(2,1)S(1)}, bf16[256,256]{1,0:T(8,128)(2,1)S(1)}, u32[]{:S(2)}, u32[]{:S(2)}) collective-permute-start(bf16[256,256]{1,0:T(8,128)(2,1)S(1)} %collective-permute-done.5.refs_6_), channel_id=1, source_target_pairs={{0,4},{4,0},{8,12},{12,8},{16,20},{20,16},{24,28},{28,24},{1,5},{5... | collective-permute-start | bytes 393224 | tf_op jit(solution)/shard_map/ppermute | solution.py:194
  12.9 5.0 %collective-permute-done.3.refs_4_ = bf16[256,256]{1,0:T(8,128)(2,1)S(1)} collective-permute-done((bf16[256,256]{1,0:T(8,128)(2,1)S(1)}, bf16[256,256]{1,0:T(8,128)(2,1)S(1)}, u32[]{:S(2)}, u32[]{:S(2)}) %collective-permute-start.3) | collective-permute-done | bytes 131104 | tf_op jit(solution)/shard_map/ppermute | solution.py:194
  17.8 1.5 %collective-permute-start.4 = (bf16[256,256]{1,0:T(8,128)(2,1)S(1)}, bf16[256,256]{1,0:T(8,128)(2,1)S(1)}, u32[]{:S(2)}, u32[]{:S(2)}) collective-permute-start(bf16[256,256]{1,0:T(8,128)(2,1)S(1)} %collective-permute-done.3.refs_4_), channel_id=1, source_target_pairs={{0,4},{4,0},{8,12},{12,8},{16,20},{20,16},{24,28},{28,24},{1,5},{5... | collective-permute-start | bytes 393224 | tf_op jit(solution)/shard_map/ppermute | solution.py:194
  19.3 0.0 collective-permute-done.1.refs_2_
  19.3 0.5 %collective-permute-start.2 = (bf16[256,256]{1,0:T(8,128)(2,1)S(1)}, bf16[256,256]{1,0:T(8,128)(2,1)S(1)}, u32[]{:S(2)}, u32[]{:S(2)}) collective-permute-start(bf16[256,256]{1,0:T(8,128)(2,1)S(1)} %collective-permute-done.1.refs_2_), channel_id=1, source_target_pairs={{0,4},{4,0},{8,12},{12,8},{16,20},{20,16},{24,28},{28,24},{1,5},{5... | collective-permute-start | bytes 393224 | tf_op jit(solution)/shard_map/ppermute | solution.py:194
  19.9 0.0 collective-permute-done.refs_1_
  19.9 0.0 collective-permute-done.6.refs_7_
  19.9 3.9 %collective-permute-done.4.refs_5_ = bf16[256,256]{1,0:T(8,128)(2,1)S(1)} collective-permute-done((bf16[256,256]{1,0:T(8,128)(2,1)S(1)}, bf16[256,256]{1,0:T(8,128)(2,1)S(1)}, u32[]{:S(2)}, u32[]{:S(2)}) %collective-permute-start.4) | collective-permute-done | bytes 131104 | tf_op jit(solution)/shard_map/ppermute | solution.py:194
  23.8 1.4 %collective-permute-done.2.refs_3_ = bf16[256,256]{1,0:T(8,128)(2,1)S(1)} collective-permute-done((bf16[256,256]{1,0:T(8,128)(2,1)S(1)}, bf16[256,256]{1,0:T(8,128)(2,1)S(1)}, u32[]{:S(2)}, u32[]{:S(2)}) %collective-permute-start.2) | collective-permute-done | bytes 131104 | tf_op jit(solution)/shard_map/ppermute | solution.py:194
  25.2 0.0 copy-start
  25.2 1.0 %copy-done = bf16[128,2048]{1,0:T(8,128)(2,1)S(1)} copy-done((bf16[128,2048]{1,0:T(8,128)(2,1)S(1)}, bf16[128,2048]{1,0:T(8,128)(2,1)}, u32[]{:S(2)}) %copy-start) | copy-done | bytes 524312
  26.3 0.0 copy-start.1
  26.3 0.7 %copy-done.1 = s32[8]{0:T(128)S(1)} copy-done((s32[8]{0:T(128)S(1)}, s32[8]{0:T(128)}, u32[]{:S(2)}) %copy-start.1) | copy-done | bytes 56
  26.9 0.0 copy-start.2
  26.9 0.7 %copy-done.2 = s32[4]{0:T(128)S(1)} copy-done((s32[4]{0:T(128)S(1)}, s32[4]{0:T(128)}, u32[]{:S(2)}) %copy-start.2) | copy-done | bytes 40
  27.6 7.0 %attend_project.1 = (bf16[64,4096]{1,0:T(8,128)(2,1)S(1)}, f32[64,4096]{1,0:T(8,128)S(1)}) custom-call(s32[8]{0:T(128)S(1)} %copy-done.1, s32[4]{0:T(128)S(1)} %copy-done.2, bf16[128,2048]{1,0:T(8,128)(2,1)S(1)} %copy-done, bf16[256,256]{1,0:T(8,128)(2,1)S(1)} %constant_dynamic-update-slice_fusion.refs_0_, ...), custom_call_target="tpu_custom_call" | custom-call | flops 2147483648 | bytes 16777216 | tf_op jit(solution)/shard_map/attend_project/pallas_call | solution.py:212
  34.6 0.1 collective-permute-start.7
  34.7 1.9 %collective-permute-done.7 = bf16[64,4096]{1,0:T(8,128)(2,1)S(1)} collective-permute-done((bf16[64,4096]{1,0:T(8,128)(2,1)S(1)}, bf16[64,4096]{1,0:T(8,128)(2,1)S(1)}, u32[]{:S(2)}, u32[]{:S(2)}) %collective-permute-start.7) | collective-permute-done | bytes 524320 | tf_op jit(solution)/shard_map/ppermute | solution.py:235
  36.6 0.1 add_convert_fusion.1
  36.7 1.6 %collective-permute-start.8 = (bf16[32,4096]{1,0:T(8,128)(2,1)S(1)}, bf16[32,4096]{1,0:T(8,128)(2,1)S(1)}, u32[]{:S(2)}, u32[]{:S(2)}) collective-permute-start(bf16[32,4096]{1,0:T(8,128)(2,1)S(1)} %add_convert_fusion.1), channel_id=1, source_target_pairs={{0,2},{1,3},{2,0},{3,1},{4,6},{5,7},{6,4},{7,5},{8,10},{9,11},{10,... | collective-permute-start | bytes 786440 | tf_op jit(solution)/shard_map/ppermute | solution.py:238
  38.2 6.8 %collective-permute-done.8 = bf16[32,4096]{1,0:T(8,128)(2,1)S(1)} collective-permute-done((bf16[32,4096]{1,0:T(8,128)(2,1)S(1)}, bf16[32,4096]{1,0:T(8,128)(2,1)S(1)}, u32[]{:S(2)}, u32[]{:S(2)}) %collective-permute-start.8) | collective-permute-done | bytes 262176 | tf_op jit(solution)/shard_map/ppermute | solution.py:238
  45.1 0.8 %add_convert_fusion = bf16[32,4096]{1,0:T(8,128)(2,1)} fusion(bf16[32,4096]{1,0:T(8,128)(2,1)S(1)} %collective-permute-done.8, f32[64,4096]{1,0:T(8,128)S(1)} %get-tuple-element.7, bf16[64,4096]{1,0:T(8,128)(2,1)S(1)} %collective-permute-done.7), kind=kLoop, calls=%fused_computation | loop fusion | flops 655360 | bytes 1310720 | tf_op jit(solution)/shard_map/convert_element_type | solution.py:239
Async XLA Ops:
  1.7 9.5 %collective-permute-start.5 = (bf16[256,256]{1,0:T(8,128)(2,1)S(1)}, bf16[256,256]{1,0:T(8,128)(2,1)S(1)}, u32[]{:S(2)}, u32[]{:S(2)}) collective-permute-start(bf16[256,256]{1,0:T(8,128)(2,1)S(1)} %constant_dynamic-update-slice_fusion.refs_0_), channel_id=1, source_target_pairs={{0,24},{4,28},{8,16},{12,20},{16,8},{20,12},{24,0},{28,4},{1,25},{... | collective-permute-start | bytes 393224 | tf_op jit(solution)/shard_map/ppermute | solution.py:194
  6.8 11.1 %collective-permute-start.3 = (bf16[256,256]{1,0:T(8,128)(2,1)S(1)}, bf16[256,256]{1,0:T(8,128)(2,1)S(1)}, u32[]{:S(2)}, u32[]{:S(2)}) collective-permute-start(bf16[256,256]{1,0:T(8,128)(2,1)S(1)} %constant_dynamic-update-slice_fusion.refs_0_), channel_id=1, source_target_pairs={{0,16},{4,20},{8,24},{12,28},{16,0},{20,4},{24,8},{28,12},{1,17},{... | collective-permute-start | bytes 393224 | tf_op jit(solution)/shard_map/ppermute | solution.py:194
  6.8 12.6 %collective-permute-start.1 = (bf16[256,256]{1,0:T(8,128)(2,1)S(1)}, bf16[256,256]{1,0:T(8,128)(2,1)S(1)}, u32[]{:S(2)}, u32[]{:S(2)}) collective-permute-start(bf16[256,256]{1,0:T(8,128)(2,1)S(1)} %constant_dynamic-update-slice_fusion.refs_0_), channel_id=1, source_target_pairs={{0,8},{4,12},{8,0},{12,4},{16,24},{20,28},{24,16},{28,20},{1,9},{5... | collective-permute-start | bytes 393224 | tf_op jit(solution)/shard_map/ppermute | solution.py:194
  7.3 12.5 %collective-permute-start = (bf16[256,256]{1,0:T(8,128)(2,1)S(1)}, bf16[256,256]{1,0:T(8,128)(2,1)S(1)}, u32[]{:S(2)}, u32[]{:S(2)}) collective-permute-start(bf16[256,256]{1,0:T(8,128)(2,1)S(1)} %constant_dynamic-update-slice_fusion.refs_0_), channel_id=1, source_target_pairs={{0,4},{4,0},{8,12},{12,8},{16,20},{20,16},{24,28},{28,24},{1,5},{5... | collective-permute-start | bytes 393224 | tf_op jit(solution)/shard_map/ppermute | solution.py:194
  11.2 8.7 %collective-permute-start.6 = (bf16[256,256]{1,0:T(8,128)(2,1)S(1)}, bf16[256,256]{1,0:T(8,128)(2,1)S(1)}, u32[]{:S(2)}, u32[]{:S(2)}) collective-permute-start(bf16[256,256]{1,0:T(8,128)(2,1)S(1)} %collective-permute-done.5.refs_6_), channel_id=1, source_target_pairs={{0,4},{4,0},{8,12},{12,8},{16,20},{20,16},{24,28},{28,24},{1,5},{5... | collective-permute-start | bytes 393224 | tf_op jit(solution)/shard_map/ppermute | solution.py:194
  17.8 6.0 %collective-permute-start.4 = (bf16[256,256]{1,0:T(8,128)(2,1)S(1)}, bf16[256,256]{1,0:T(8,128)(2,1)S(1)}, u32[]{:S(2)}, u32[]{:S(2)}) collective-permute-start(bf16[256,256]{1,0:T(8,128)(2,1)S(1)} %collective-permute-done.3.refs_4_), channel_id=1, source_target_pairs={{0,4},{4,0},{8,12},{12,8},{16,20},{20,16},{24,28},{28,24},{1,5},{5... | collective-permute-start | bytes 393224 | tf_op jit(solution)/shard_map/ppermute | solution.py:194
  19.3 5.9 %collective-permute-start.2 = (bf16[256,256]{1,0:T(8,128)(2,1)S(1)}, bf16[256,256]{1,0:T(8,128)(2,1)S(1)}, u32[]{:S(2)}, u32[]{:S(2)}) collective-permute-start(bf16[256,256]{1,0:T(8,128)(2,1)S(1)} %collective-permute-done.1.refs_2_), channel_id=1, source_target_pairs={{0,4},{4,0},{8,12},{12,8},{16,20},{20,16},{24,28},{28,24},{1,5},{5... | collective-permute-start | bytes 393224 | tf_op jit(solution)/shard_map/ppermute | solution.py:194
  25.2 1.0 %copy-start = (bf16[128,2048]{1,0:T(8,128)(2,1)S(1)}, bf16[128,2048]{1,0:T(8,128)(2,1)}, u32[]{:S(2)}) copy-start(bf16[128,2048]{1,0:T(8,128)(2,1)} %q_ref.1) | copy-start | bytes 1572868
  26.3 0.7 %copy-start.1 = (s32[8]{0:T(128)S(1)}, s32[8]{0:T(128)}, u32[]{:S(2)}) copy-start(s32[8]{0:T(128)} %order_ref.1) | copy-start | bytes 100
  26.9 0.7 %copy-start.2 = (s32[4]{0:T(128)S(1)}, s32[4]{0:T(128)}, u32[]{:S(2)}) copy-start(s32[4]{0:T(128)} %docs_ref.1) | copy-start | bytes 52
  34.6 2.0 %collective-permute-start.7 = (bf16[64,4096]{1,0:T(8,128)(2,1)S(1)}, bf16[64,4096]{1,0:T(8,128)(2,1)S(1)}, u32[]{:S(2)}, u32[]{:S(2)}) collective-permute-start(bf16[64,4096]{1,0:T(8,128)(2,1)S(1)} %get-tuple-element.8), channel_id=1, source_target_pairs={{0,1},{1,0},{2,3},{3,2},{4,5},{5,4},{6,7},{7,6},{8,9},{9,8},{10,11... | collective-permute-start | bytes 1572872 | tf_op jit(solution)/shard_map/ppermute | solution.py:235
  36.7 8.4 %collective-permute-start.8 = (bf16[32,4096]{1,0:T(8,128)(2,1)S(1)}, bf16[32,4096]{1,0:T(8,128)(2,1)S(1)}, u32[]{:S(2)}, u32[]{:S(2)}) collective-permute-start(bf16[32,4096]{1,0:T(8,128)(2,1)S(1)} %add_convert_fusion.1), channel_id=1, source_target_pairs={{0,2},{1,3},{2,0},{3,1},{4,6},{5,7},{6,4},{7,5},{8,10},{9,11},{10,... | collective-permute-start | bytes 786440 | tf_op jit(solution)/shard_map/ppermute | solution.py:238

commit v2 on v0

--- a/solution.py
+++ b/solution.py
@@ -1,13 +1,17 @@
+import functools
+
 import jax
 import jax.numpy as jnp
 from jax import lax
+from jax.experimental import pallas as pl
+from jax.experimental.pallas import tpu as pltpu
 from jax.sharding import PartitionSpec as P
+
 
 HEAD_SIZE = 128
 BLOCK_TOKENS = 128
-
-
-document_masked_score = -1e30
+MASKED = -1e30
+SCALE = HEAD_SIZE**-0.5 * 1.4426950408889634
 
 
 def lookup(entries, indices):
@@ -28,7 +32,7 @@
     scores = jnp.einsum(
         "qhgd,khd->hgqk", query_rows, key_rows, preferred_element_type=jnp.float32
     ) * HEAD_SIZE ** (-0.5)
-    scores = jnp.where(allowed, scores, document_masked_score)
+    scores = jnp.where(allowed, scores, MASKED)
     new_max = jnp.maximum(running_max, jnp.max(scores, axis=-1))
     weights = jnp.where(allowed, jnp.exp(scores - new_max[..., None]), 0.0)
     factor = jnp.exp(running_max - new_max)
@@ -47,26 +51,14 @@
 ):
     length = key_part.shape[0]
     heads_kv = key_part.shape[1] // HEAD_SIZE
-    block_rows = 512
+    block_rows = 4 * BLOCK_TOKENS
     token_blocks = length // block_rows
     key_pos, key_doc = locate(jnp.arange(length, dtype=jnp.int32), block_order, doc_ends)
 
     def scan_step(status, pieces_now):
-        return (
-            attend(
-                status,
-                pieces_now[0],
-                pieces_now[1],
-                pieces_now[2],
-                pieces_now[3],
-                query_rows,
-                query_pos,
-                query_doc,
-            ),
-            None,
-        )
-
-    online, unused = lax.scan(
+        return attend(status, *pieces_now, query_rows, query_pos, query_doc), None
+
+    online, _ = lax.scan(
         scan_step,
         online,
         (
@@ -79,7 +71,7 @@
     return online
 
 
-def local(queries, keys, values, doc_blocks, block_order, out_weight):
+def general(queries, keys, values, doc_blocks, block_order, out_weight):
     rows_dev = queries.shape[0]
     heads_kv = keys.shape[1] // HEAD_SIZE
     group_size = queries.shape[1] // keys.shape[1]
@@ -90,39 +82,277 @@
     )
     query_rows = queries.reshape(rows_dev, heads_kv, group_size, HEAD_SIZE)
     starting_state = (
-        jnp.full((heads_kv, group_size, rows_dev), document_masked_score, jnp.float32),
+        jnp.full((heads_kv, group_size, rows_dev), MASKED, jnp.float32),
         jnp.zeros((heads_kv, group_size, rows_dev), jnp.float32),
         jnp.zeros((heads_kv, group_size, rows_dev, HEAD_SIZE), jnp.float32),
     )
-    whole_keys, whole_values = (
-        lax.all_gather(keys, "cp", axis=0, tiled=True),
-        lax.all_gather(values, "cp", axis=0, tiled=True),
-    )
-    running_max, weight_sum, weighted = sweep_keys(
-        starting_state,
-        whole_keys,
-        whole_values,
-        block_order,
-        doc_ends,
-        query_rows,
-        query_pos,
-        query_doc,
+    whole_keys = lax.all_gather(keys, "cp", axis=0, tiled=True)
+    whole_values = lax.all_gather(values, "cp", axis=0, tiled=True)
+    _, weight_sum, weighted = sweep_keys(
+        starting_state, whole_keys, whole_values, block_order, doc_ends,
+        query_rows, query_pos, query_doc,
     )
     attended = (
         jnp.transpose(weighted / weight_sum[..., None], (2, 0, 1, 3))
         .reshape(rows_dev, -1)
         .astype(jnp.bfloat16)
     )
-    summed = lax.psum_scatter(
+    return lax.psum_scatter(
         jnp.dot(attended, out_weight, preferred_element_type=jnp.float32).astype(jnp.bfloat16),
         "tp",
         scatter_dimension=0,
         tiled=True,
     )
-    return summed
+
+
+def spread(x, width):
+    return jnp.concatenate([x] * (width // x.shape[1]), 1)
+
+
+def online(top_ref, sum_ref, at, queries, key_rows, value_rows, bias, fresh=False):
+    scores = lax.dot_general(
+        queries, key_rows, (((1,), (1,)), ((), ())), preferred_element_type=jnp.float32
+    )
+    if bias is not None:
+        scores = scores + bias
+    top = jnp.broadcast_to(jnp.max(scores, axis=1, keepdims=True), (scores.shape[0], HEAD_SIZE))
+    if not fresh:
+        before = top_ref[at, :]
+        top = jnp.maximum(top, before)
+    weights = jnp.exp2((scores - spread(top, scores.shape[1])) * SCALE).astype(jnp.bfloat16)
+    sums = jnp.dot(weights, value_rows, preferred_element_type=jnp.float32)
+    if not fresh:
+        sums = sums + sum_ref[at, :] * spread(jnp.exp2((before - top) * SCALE), sums.shape[1])
+    top_ref[at, :] = top
+    sum_ref[at, :] = sums
+
+
+def sweep(qr_ref, top_ref, sum_ref, kvs, bias, fresh=False, pieces=2):
+    heads_kv = kvs[0].shape[1] // HEAD_SIZE
+    height = qr_ref.shape[0] // heads_kv
+    for g in range(heads_kv):
+        cols = slice(g * HEAD_SIZE, (g + 1) * HEAD_SIZE)
+        key_rows = jnp.concatenate([ref[:BLOCK_TOKENS, cols] for ref in kvs], 0)
+        value_rows = jnp.concatenate([ref[BLOCK_TOKENS:, cols] for ref in kvs], 0)
+        value_rows = jnp.concatenate([value_rows, jnp.ones_like(value_rows)], 1)
+        for i in range(pieces):
+            at = pl.ds(g * height + i * (height // pieces), height // pieces)
+            online(top_ref, sum_ref, at, qr_ref[at, :], key_rows, value_rows, bias, fresh)
+
+
+def start_all(copies):
+    for copy in copies:
+        copy.start()
+    return copies
+
+
+def wait_all(copies):
+    for copy in copies:
+        copy.wait()
+
+
+def load_rows(src, first, out, sems):
+    pieces = sems.shape[0]
+    rows = out.shape[0] // pieces
+    return start_all([
+        pltpu.make_async_copy(
+            src.at[pl.ds(first + i * rows, rows)], out.at[pl.ds(i * rows, rows)], sems.at[i])
+        for i in range(pieces)
+    ])
+
+
+def begin(n_tp, order_hbm, docs_hbm, q_hbm, w_hbm, kv_ref, qr_ref, seen_ref, top_ref, sum_ref, w_ref,
+          q_ref, order_ref, docs_ref, sems, w_sems):
+    copies = start_all([
+        pltpu.make_async_copy(src, dst, sems.at[i])
+        for i, (src, dst) in enumerate(
+            ((order_hbm, order_ref), (docs_hbm, docs_ref), (q_hbm, q_ref)))
+    ])
+    loads = load_rows(w_hbm, 0, w_ref, w_sems)
+    wait_all(copies)
+    n_blocks, n_docs = order_ref.shape[0], docs_ref.shape[0]
+    rows, width = q_ref.shape
+    part = rows // n_tp
+    me, core = lax.axis_index("cp"), lax.axis_index("tp")
+    ends = []
+    for d in range(n_docs):
+        ends.append(docs_ref[d] + (ends[-1] if ends else 0))
+
+    def document(seq):
+        return sum((seq >= end).astype(jnp.int32) for end in ends)
+
+    own_seq = order_ref[me]
+    own_doc = document(own_seq)
+    for s in range(n_blocks):
+        seq = order_ref[me ^ s]
+        seen = (document(seq) == own_doc) & (seq < own_seq)
+        seen_ref[s : s + 1, :] = jnp.full((1, HEAD_SIZE), seen.astype(jnp.int32), jnp.int32)
+
+    targets = [core ^ f for f in (3, 1, 2, 0)]
+    for h in range(width // HEAD_SIZE):
+        for p, target in enumerate(targets):
+            qr_ref[h * rows + p * part : h * rows + (p + 1) * part, :] = q_ref[
+                pl.ds(pl.multiple_of(target * part, part), part),
+                h * HEAD_SIZE : (h + 1) * HEAD_SIZE]
+    key_at = lax.broadcasted_iota(jnp.int32, (part, BLOCK_TOKENS), 1)
+    row_at = lax.broadcasted_iota(jnp.int32, (part, BLOCK_TOKENS), 0)
+    bias = jnp.concatenate(
+        [jnp.where(key_at <= row_at + target * part, 0.0, MASKED) for target in targets], 0)
+    heads = width // kv_ref.shape[1]
+    sweep(qr_ref, top_ref, sum_ref, [kv_ref], jnp.concatenate([bias] * (heads // 2), 0), fresh=True)
+    wait_all(loads)
+
+
+def seen_blocks(slots, seen_hbm, seen_smem, sem, qr_ref, top_ref, sum_ref, kv_refs, kv_ref):
+    wait_all(start_all([pltpu.make_async_copy(seen_hbm, seen_smem, sem)]))
+    used = jnp.int32(0)
+    for s, ref in zip(slots, kv_refs):
+        wanted = seen_smem[s, 0]
+
+        @pl.when(wanted == 1)
+        def _(ref=ref, used=used):
+            kv_ref[used] = ref[...]
+
+        used = used + wanted
+    for first in range(0, kv_ref.shape[0], 2):
+        for count in (1, 2):
+            if first + count > kv_ref.shape[0]:
+                continue
+
+            @pl.when((used >= first + 2) if count == 2 else (used == first + 1))
+            def _(first=first, count=count):
+                sweep(qr_ref, top_ref, sum_ref, [kv_ref.at[first + i] for i in range(count)], None)
+
+
+def more(slots, seen_ref, w_hbm, qr_ref, top_in, sum_in, *refs):
+    kv_refs, (top_ref, sum_ref, w_ref, kv_ref, seen_smem, sem, w_sems) = (
+        refs[: len(slots)], refs[len(slots) :])
+    loads = load_rows(w_hbm, w_ref.shape[0], w_ref, w_sems)
+    seen_blocks(slots, seen_ref, seen_smem, sem, qr_ref, top_ref, sum_ref, kv_refs, kv_ref)
+    wait_all(loads)
+
+
+def finish(slots, chunk, seen_ref, qr_ref, top_in, sum_in, *refs):
+    kv_refs, (w0_ref, w1_ref, top_ref, sum_ref, give_ref, keep_ref, att_ref, kv_ref, seen_smem, sem) = (
+        refs[: len(slots)], refs[len(slots) :])
+    seen_blocks(slots, seen_ref, seen_smem, sem, qr_ref, top_ref, sum_ref, kv_refs, kv_ref)
+    rows, width = att_ref.shape
+    for h in range(width // HEAD_SIZE):
+        at = slice(h * rows, (h + 1) * rows)
+        att_ref[:, h * HEAD_SIZE : (h + 1) * HEAD_SIZE] = (
+            sum_ref[at, :HEAD_SIZE] / sum_ref[at, HEAD_SIZE:]
+        ).astype(jnp.bfloat16)
+    depth = w0_ref.shape[0]
+    for j in range(w0_ref.shape[1] // chunk):
+        cols = slice(j * chunk, (j + 1) * chunk)
+        product = jnp.dot(att_ref[:, :depth], w0_ref[:, cols], preferred_element_type=jnp.float32)
+        product += jnp.dot(att_ref[:, depth:], w1_ref[:, cols], preferred_element_type=jnp.float32)
+        give_ref[:, cols] = product[: rows // 2].astype(jnp.bfloat16)
+        keep_ref[:, cols] = product[rows // 2 :]
+
+
+def in_hbm(x):
+    return pltpu.with_memory_space_constraint(x, pltpu.HBM)
+
+
+def in_vmem(x):
+    return pltpu.with_memory_space_constraint(x, pltpu.VMEM)
+
+
+HBM = pl.BlockSpec(memory_space=pltpu.HBM)
+VMEM = pl.BlockSpec(memory_space=pltpu.VMEM)
+
+
+def kernel(body, inputs, outs, scratch=(), flops=0, aliases={}, limit=16):
+    return pl.pallas_call(
+        body,
+        out_shape=tuple(pltpu.VMEM(shape, dtype) for shape, dtype in outs),
+        in_specs=[HBM if where == "hbm" else VMEM for where, _ in inputs],
+        out_specs=(VMEM,) * len(outs),
+        scratch_shapes=list(scratch),
+        input_output_aliases=aliases,
+        compiler_params=pltpu.CompilerParams(vmem_limit_bytes=limit * 1024 * 1024),
+        cost_estimate=pl.CostEstimate(flops=flops, bytes_accessed=0, transcendentals=0),
+    )(*[in_hbm(x) if where == "hbm" else in_vmem(x) for where, x in inputs])
+
+
+def stack_kernel(k_hbm, v_hbm, out_ref, sems):
+    rows = k_hbm.shape[0]
+    copies = [
+        pltpu.make_async_copy(k_hbm, out_ref.at[:rows], sems.at[0]),
+        pltpu.make_async_copy(v_hbm, out_ref.at[rows:], sems.at[1]),
+    ]
+    for copy in copies:
+        copy.start()
+    for copy in copies:
+        copy.wait()
+
+
+PLAN = ((4, 0, 4), (2, 0, 2), (1, 0, 1), (7, 0, 7), (3, 2, 1), (6, 4, 2), (5, 4, 1))
+
+
+def blockwise(n, n_tp, queries, keys, values, doc_blocks, block_order, out_weight):
+    rows, width = queries.shape
+    heads = width // HEAD_SIZE
+    out_width = out_weight.shape[1]
+    bf16, f32 = jnp.bfloat16, jnp.float32
+
+    def swap(block, s):
+        return lax.ppermute(block, "cp", [(i, i ^ s) for i in range(n)])
+
+    (kv,) = kernel(
+        stack_kernel, [("hbm", keys), ("hbm", values)],
+        [((2 * rows, keys.shape[1]), bf16)], [pltpu.SemaphoreType.DMA((2,))])
+    got = {0: kv}
+    for s, via, hop in PLAN:
+        got[s] = swap(got[via], hop)
+
+    states = [((heads * rows, HEAD_SIZE), f32), ((heads * rows, 2 * HEAD_SIZE), f32)]
+    half_weight = ((width // 2, out_width), bf16)
+    dma = pltpu.SemaphoreType.DMA
+    qr, seen, top, sums, weight0 = kernel(
+        functools.partial(begin, n_tp),
+        [("hbm", block_order), ("hbm", doc_blocks), ("hbm", queries), ("hbm", out_weight), ("vmem", kv)],
+        [((heads * rows, HEAD_SIZE), bf16), ((n, HEAD_SIZE), jnp.int32)] + states + [half_weight],
+        [pltpu.VMEM((rows, width), bf16), pltpu.SMEM(block_order.shape, jnp.int32),
+         pltpu.SMEM(doc_blocks.shape, jnp.int32), dma((3,)), dma((8,))],
+        flops=4 * 10**9, limit=8)
+    small = [pltpu.SMEM((n, HEAD_SIZE), jnp.int32), dma(())]
+
+    def held(slots):
+        return pltpu.VMEM((min(len(slots), n // 2 - 1),) + kv.shape, bf16)
+
+    slots = (1, 2, 4)
+    top, sums, weight1 = kernel(
+        functools.partial(more, slots),
+        [("vmem", seen), ("hbm", out_weight)]
+        + [("vmem", x) for x in (qr, top, sums, *(got[s] for s in slots))],
+        states + [half_weight], [held(slots)] + small + [dma((8,))],
+        flops=4 * 10**9, aliases={3: 0, 4: 1}, limit=8)
+    slots = (3, 7, 6, 5)
+    _, _, give, keep = kernel(
+        functools.partial(finish, slots, 512),
+        [("vmem", x) for x in (seen, qr, top, sums, *(got[s] for s in slots), weight0, weight1)],
+        states + [((rows // 2, out_width), bf16), ((rows // 2, out_width), f32)],
+        [pltpu.VMEM((rows, width), bf16), held(slots)] + small,
+        flops=2 * rows * width * out_width, aliases={2: 0, 3: 1}, limit=8)
+    part = rows // n_tp
+    got = lax.ppermute(give, "tp", [(i, i ^ 1) for i in range(n_tp)])
+    far = (keep[:part] + got[:part].astype(f32)).astype(bf16)
+    near = keep[part:] + got[part:].astype(f32)
+    crossed = lax.ppermute(far, "tp", [(i, i ^ 2) for i in range(n_tp)])
+    return (near + crossed.astype(f32)).astype(bf16)
 
 
 def solution(mesh):
+    n, n_tp = mesh.shape["cp"], mesh.shape["tp"]
+
+    def local(queries, keys, values, doc_blocks, block_order, out_weight):
+        args = (queries, keys, values, doc_blocks, block_order, out_weight)
+        if n == 8 and n_tp == 4:
+            return blockwise(n, n_tp, *args)
+        return general(*args)
+
     placed = (P("cp", "tp"), P("cp", "tp"), P("cp", "tp"), P(), P(), P("tp", None))
     return jax.shard_map(
         local, mesh=mesh, in_specs=placed, out_specs=P(("cp", "tp"), None), check_vma=False

time: 127 us -> 41.2 us (0.32)
  blocking collectives: 64.8 us -> 0 us
  matrix products: 14.1 us -> 0 us
  between operations: 13.5 us -> 0.06 us
  Pallas kernels: 0 us -> 13.2 us
  starting transfers between devices: 0.01 us -> 11 us
  waiting for transfers between devices: 26.2 us -> 16 us
  other arithmetic: 5.09 us -> 0.83 us
  local copies, waits for them, and re-layouts: 2.96 us -> 0 us
    all_gather x2 -> x0, blocking collectives: 64.8 us -> none  [the longest x1 33.3 us: local(): lax.all_gather(keys, 'cp', axis=0, tiled=True)]
    reduce_scatter x1 -> x0, waiting for transfers between devices: 26.1 us -> none  [local(): lax.psum_scatter(jnp.dot(attended, out_weight, preferred_element_type=jnp...]
    ppermute x0 -> x9, waiting for transfers between devices: none -> 16 us  [the longest x7 7.29 us: swap(): return lax.ppermute(block, 'cp', [(i, i ^ s) for i in range(n)])]
    dot_general x5 -> x0, matrix products: 14.1 us -> none  [the longest x1 9.15 us: local(): jnp.dot(attended, out_weight, preferred_element_type=jnp.float32)]
    pallas_call x0 -> x4, Pallas kernels: none -> 13.2 us  [kernel(): pl.pallas_call(body, out_shape=tuple((pltpu.VMEM(shape, dtype) for shape,...]
    ppermute x0 -> x9, starting transfers between devices: none -> 11 us  [the longest x7 9.31 us: swap(): return lax.ppermute(block, 'cp', [(i, i ^ s) for i in range(n)])]
    reduce_sum x6 -> x0, other arithmetic: 3.65 us -> none  [the longest x2 2.01 us: attend(): weight_sum = weight_sum * factor + jnp.sum(weights, axis=-1)]
    unnamed x2 -> x0, local copies, waits for them, and re-layouts: 1.6 us -> none
  transfers between devices with their start and end apart: 1 -> 9, of which waited for: 1 -> 5; matrix products, arithmetic and copies ran while one was open for 0% -> 0% of each run, Pallas kernels for 0% -> 19%
where the time goes in v2:
time: 41.2 us; the launch traced here: 41 us
  waiting for transfers between devices  16 us (39%)
  Pallas kernels  13.2 us (32%)
  starting transfers between devices  11 us (27%)
  other arithmetic  0.83 us (2%)
    pallas_call x4, Pallas kernels, kernel(): pl.pallas_call(body, out_shape=tuple((pltpu.VMEM(shape, dtype) for shape,...  13.2 us
    ppermute x7, starting transfers between devices, swap(): return lax.ppermute(block, 'cp', [(i, i ^ s) for i in range(n)])  9.31 us
    ppermute x7, waiting for transfers between devices, swap(): return lax.ppermute(block, 'cp', [(i, i ^ s) for i in range(n)])  7.29 us
    ppermute x1, waiting for transfers between devices, blockwise(): crossed = lax.ppermute(far, 'tp', [(i, i ^ 2) for i in range(n_tp)])  6.83 us
    ppermute x1, waiting for transfers between devices, blockwise(): got = lax.ppermute(give, 'tp', [(i, i ^ 1) for i in range(n_tp)])  1.9 us
    ppermute x1, starting transfers between devices, blockwise(): crossed = lax.ppermute(far, 'tp', [(i, i ^ 2) for i in range(n_tp)])  1.58 us
  transfers between devices with their start and end apart: 9, of which 5 were waited for; matrix products, arithmetic and copies ran while one was open for 0% of the time, Pallas kernels for 19%

profile of v2, /device:TPU:0, one launch (start us, length us, event | category | flops | bytes accessed | tf_op | source)
XLA Modules:
  0.0 41.0 jit_solution(3354767024837902262)
XLA Ops:
  0.0 0.9 %shard_map.64.kv_ref = bf16[256,256]{1,0:T(8,128)(2,1)S(1)} custom-call(bf16[128,256]{1,0:T(8,128)(2,1)} %k_hbm.1, bf16[128,256]{1,0:T(8,128)(2,1)} %v_hbm.1), custom_call_target="tpu_custom_call" | custom-call | tf_op jit(solution)/shard_map/pallas_call | solution.py:267
  0.9 6.1 %collective-permute-start.4 = (bf16[256,256]{1,0:T(8,128)(2,1)S(1)}, bf16[256,256]{1,0:T(8,128)(2,1)S(1)}, u32[]{:S(2)}, u32[]{:S(2)}) collective-permute-start(bf16[256,256]{1,0:T(8,128)(2,1)S(1)} %shard_map.64.kv_ref), channel_id=1, source_target_pairs={{0,28},{4,24},{8,20},{12,16},{16,12},{20,8},{24,4},{28,0},{1,29},{... | collective-permute-start | bytes 393224 | tf_op jit(solution)/shard_map/ppermute | solution.py:301
  7.0 0.0 collective-permute-start.2
  7.0 0.8 %collective-permute-start.1 = (bf16[256,256]{1,0:T(8,128)(2,1)S(1)}, bf16[256,256]{1,0:T(8,128)(2,1)S(1)}, u32[]{:S(2)}, u32[]{:S(2)}) collective-permute-start(bf16[256,256]{1,0:T(8,128)(2,1)S(1)} %shard_map.64.kv_ref), channel_id=1, source_target_pairs={{0,8},{4,12},{8,0},{12,4},{16,24},{20,28},{24,16},{28,20},{1,9},{5... | collective-permute-start | bytes 393224 | tf_op jit(solution)/shard_map/ppermute | solution.py:301
  7.8 0.4 %collective-permute-start = (bf16[256,256]{1,0:T(8,128)(2,1)S(1)}, bf16[256,256]{1,0:T(8,128)(2,1)S(1)}, u32[]{:S(2)}, u32[]{:S(2)}) collective-permute-start(bf16[256,256]{1,0:T(8,128)(2,1)S(1)} %shard_map.64.kv_ref), channel_id=1, source_target_pairs={{0,4},{4,0},{8,12},{12,8},{16,20},{20,16},{24,28},{28,24},{1,5},{5... | collective-permute-start | bytes 393224 | tf_op jit(solution)/shard_map/ppermute | solution.py:301
  8.2 4.5 %shard_map.65 = (bf16[2048,128]{1,0:T(8,128)(2,1)S(1)}, s32[8,128]{1,0:T(8,128)S(1)}, f32[2048,128]{1,0:T(8,128)S(1)}, f32[2048,256]{1,0:T(8,128)S(1)}, bf16[1024,4096]{1,0:T(8,128)(2,1)S(1)}) custom-call(s32[8]{0:T(128)} %order_hbm.1, s32[4]{0:T(128)} %docs_hbm.1, bf16[128,2048]{1,0:T(8,128)(2,1)} %q_hbm.1, bf16[2048,4096]{1,0:T(8,128)(2,1)} %w_hbm.3, ...), custom_call_target="tpu_custom_call" | custom-call | flops 4000000000 | tf_op jit(solution)/shard_map/pallas_call | solution.py:267
  12.7 5.4 %collective-permute-done.2.refs_2_ = bf16[256,256]{1,0:T(8,128)(2,1)S(1)} collective-permute-done((bf16[256,256]{1,0:T(8,128)(2,1)S(1)}, bf16[256,256]{1,0:T(8,128)(2,1)S(1)}, u32[]{:S(2)}, u32[]{:S(2)}) %collective-permute-start.2) | collective-permute-done | bytes 131104 | tf_op jit(solution)/shard_map/ppermute | solution.py:301
  18.0 0.5 %collective-permute-start.6 = (bf16[256,256]{1,0:T(8,128)(2,1)S(1)}, bf16[256,256]{1,0:T(8,128)(2,1)S(1)}, u32[]{:S(2)}, u32[]{:S(2)}) collective-permute-start(bf16[256,256]{1,0:T(8,128)(2,1)S(1)} %collective-permute-done.2.refs_2_), channel_id=1, source_target_pairs={{0,4},{4,0},{8,12},{12,8},{16,20},{20,16},{24,28},{28,24},{1,5},{5... | collective-permute-start | bytes 393224 | tf_op jit(solution)/shard_map/ppermute | solution.py:301
  18.6 0.0 collective-permute-start.5
  18.6 0.0 collective-permute-done.1.refs_1_
  18.6 1.5 %collective-permute-start.3 = (bf16[256,256]{1,0:T(8,128)(2,1)S(1)}, bf16[256,256]{1,0:T(8,128)(2,1)S(1)}, u32[]{:S(2)}, u32[]{:S(2)}) collective-permute-start(bf16[256,256]{1,0:T(8,128)(2,1)S(1)} %collective-permute-done.1.refs_1_), channel_id=1, source_target_pairs={{0,4},{4,0},{8,12},{12,8},{16,20},{20,16},{24,28},{28,24},{1,5},{5... | collective-permute-start | bytes 393224 | tf_op jit(solution)/shard_map/ppermute | solution.py:301
  20.1 0.0 collective-permute-done.refs_0_
  20.1 3.5 %shard_map.66 = (f32[2048,128]{1,0:T(8,128)S(1)}, f32[2048,256]{1,0:T(8,128)S(1)}, bf16[1024,4096]{1,0:T(8,128)(2,1)S(1)}) custom-call(s32[8,128]{1,0:T(8,128)S(1)} %get-tuple-element.15.seen_ref, bf16[2048,4096]{1,0:T(8,128)(2,1)} %w_hbm.3, bf16[2048,128]{1,0:T(8,128)(2,1)S(1)} %get-tuple-element.16.qr_ref, ...), custom_call_target="tpu_custom_call", output_to_operand_aliasing={{0}: (3, {}), {1}: (4, {})} | custom-call | flops 4000000000 | tf_op jit(solution)/shard_map/pallas_call | solution.py:267
  23.6 0.0 collective-permute-done.4.refs_1_
  23.6 0.5 %collective-permute-done.6.refs_3_ = bf16[256,256]{1,0:T(8,128)(2,1)S(1)} collective-permute-done((bf16[256,256]{1,0:T(8,128)(2,1)S(1)}, bf16[256,256]{1,0:T(8,128)(2,1)S(1)}, u32[]{:S(2)}, u32[]{:S(2)}) %collective-permute-start.6) | collective-permute-done | bytes 131104 | tf_op jit(solution)/shard_map/ppermute | solution.py:301
  24.1 0.0 collective-permute-done.5.refs_2_
  24.1 1.4 %collective-permute-done.3.refs_0_ = bf16[256,256]{1,0:T(8,128)(2,1)S(1)} collective-permute-done((bf16[256,256]{1,0:T(8,128)(2,1)S(1)}, bf16[256,256]{1,0:T(8,128)(2,1)S(1)}, u32[]{:S(2)}, u32[]{:S(2)}) %collective-permute-start.3) | collective-permute-done | bytes 131104 | tf_op jit(solution)/shard_map/ppermute | solution.py:301
  25.5 4.3 %shard_map.67 = (f32[2048,128]{1,0:T(8,128)S(1)}, f32[2048,256]{1,0:T(8,128)S(1)}, bf16[64,4096]{1,0:T(8,128)(2,1)S(1)}, f32[64,4096]{1,0:T(8,128)S(1)}) custom-call(s32[8,128]{1,0:T(8,128)S(1)} %get-tuple-element.15.seen_ref, bf16[2048,128]{1,0:T(8,128)(2,1)S(1)} %get-tuple-element.16.qr_ref, ...), custom_call_target="tpu_custom_call", output_to_operand_aliasing={{0}: (2, {}), {1}: (3, {})} | custom-call | flops 2147483648 | tf_op jit(solution)/shard_map/pallas_call | solution.py:267
  29.8 0.1 collective-permute-start.7
  29.9 1.9 %collective-permute-done.7 = bf16[64,4096]{1,0:T(8,128)(2,1)S(1)} collective-permute-done((bf16[64,4096]{1,0:T(8,128)(2,1)S(1)}, bf16[64,4096]{1,0:T(8,128)(2,1)S(1)}, u32[]{:S(2)}, u32[]{:S(2)}) %collective-permute-start.7) | collective-permute-done | bytes 524320 | tf_op jit(solution)/shard_map/ppermute | solution.py:340
  31.8 1.6 %collective-permute-start.8 = (bf16[32,4096]{1,0:T(8,128)(2,1)S(1)}, bf16[32,4096]{1,0:T(8,128)(2,1)S(1)}, u32[]{:S(2)}, u32[]{:S(2)}) collective-permute-start(bf16[32,4096]{1,0:T(8,128)(2,1)S(1)} %add_convert_fusion.1), channel_id=1, source_target_pairs={{0,2},{1,3},{2,0},{3,1},{4,6},{5,7},{6,4},{7,5},{8,10},{9,11},{10,... | collective-permute-start | bytes 786440 | tf_op jit(solution)/shard_map/ppermute | solution.py:343
  33.4 6.8 %collective-permute-done.8 = bf16[32,4096]{1,0:T(8,128)(2,1)S(1)} collective-permute-done((bf16[32,4096]{1,0:T(8,128)(2,1)S(1)}, bf16[32,4096]{1,0:T(8,128)(2,1)S(1)}, u32[]{:S(2)}, u32[]{:S(2)}) %collective-permute-start.8) | collective-permute-done | bytes 262176 | tf_op jit(solution)/shard_map/ppermute | solution.py:343
  40.2 0.8 %add_convert_fusion = bf16[32,4096]{1,0:T(8,128)(2,1)} fusion(bf16[32,4096]{1,0:T(8,128)(2,1)S(1)} %collective-permute-done.8, f32[64,4096]{1,0:T(8,128)S(1)} %get-tuple-element.23, bf16[64,4096]{1,0:T(8,128)(2,1)S(1)} %collective-permute-done.7), kind=kLoop, calls=%fused_computation | loop fusion | flops 655360 | bytes 1310720 | tf_op jit(solution)/shard_map/convert_element_type | solution.py:344
  (1 shorter events, 0.0 us)
Async XLA Ops:
  0.9 22.7 %collective-permute-start.4 = (bf16[256,256]{1,0:T(8,128)(2,1)S(1)}, bf16[256,256]{1,0:T(8,128)(2,1)S(1)}, u32[]{:S(2)}, u32[]{:S(2)}) collective-permute-start(bf16[256,256]{1,0:T(8,128)(2,1)S(1)} %shard_map.64.kv_ref), channel_id=1, source_target_pairs={{0,28},{4,24},{8,20},{12,16},{16,12},{20,8},{24,4},{28,0},{1,29},{... | collective-permute-start | bytes 393224 | tf_op jit(solution)/shard_map/ppermute | solution.py:301
  7.0 11.1 %collective-permute-start.2 = (bf16[256,256]{1,0:T(8,128)(2,1)S(1)}, bf16[256,256]{1,0:T(8,128)(2,1)S(1)}, u32[]{:S(2)}, u32[]{:S(2)}) collective-permute-start(bf16[256,256]{1,0:T(8,128)(2,1)S(1)} %shard_map.64.kv_ref), channel_id=1, source_target_pairs={{0,16},{4,20},{8,24},{12,28},{16,0},{20,4},{24,8},{28,12},{1,17},{... | collective-permute-start | bytes 393224 | tf_op jit(solution)/shard_map/ppermute | solution.py:301
  7.0 11.6 %collective-permute-start.1 = (bf16[256,256]{1,0:T(8,128)(2,1)S(1)}, bf16[256,256]{1,0:T(8,128)(2,1)S(1)}, u32[]{:S(2)}, u32[]{:S(2)}) collective-permute-start(bf16[256,256]{1,0:T(8,128)(2,1)S(1)} %shard_map.64.kv_ref), channel_id=1, source_target_pairs={{0,8},{4,12},{8,0},{12,4},{16,24},{20,28},{24,16},{28,20},{1,9},{5... | collective-permute-start | bytes 393224 | tf_op jit(solution)/shard_map/ppermute | solution.py:301
  7.8 12.3 %collective-permute-start = (bf16[256,256]{1,0:T(8,128)(2,1)S(1)}, bf16[256,256]{1,0:T(8,128)(2,1)S(1)}, u32[]{:S(2)}, u32[]{:S(2)}) collective-permute-start(bf16[256,256]{1,0:T(8,128)(2,1)S(1)} %shard_map.64.kv_ref), channel_id=1, source_target_pairs={{0,4},{4,0},{8,12},{12,8},{16,20},{20,16},{24,28},{28,24},{1,5},{5... | collective-permute-start | bytes 393224 | tf_op jit(solution)/shard_map/ppermute | solution.py:301
  18.0 6.0 %collective-permute-start.6 = (bf16[256,256]{1,0:T(8,128)(2,1)S(1)}, bf16[256,256]{1,0:T(8,128)(2,1)S(1)}, u32[]{:S(2)}, u32[]{:S(2)}) collective-permute-start(bf16[256,256]{1,0:T(8,128)(2,1)S(1)} %collective-permute-done.2.refs_2_), channel_id=1, source_target_pairs={{0,4},{4,0},{8,12},{12,8},{16,20},{20,16},{24,28},{28,24},{1,5},{5... | collective-permute-start | bytes 393224 | tf_op jit(solution)/shard_map/ppermute | solution.py:301
  18.6 5.5 %collective-permute-start.5 = (bf16[256,256]{1,0:T(8,128)(2,1)S(1)}, bf16[256,256]{1,0:T(8,128)(2,1)S(1)}, u32[]{:S(2)}, u32[]{:S(2)}) collective-permute-start(bf16[256,256]{1,0:T(8,128)(2,1)S(1)} %collective-permute-done.2.refs_2_), channel_id=1, source_target_pairs={{0,8},{4,12},{8,0},{12,4},{16,24},{20,28},{24,16},{28,20},{1,9},{5... | collective-permute-start | bytes 393224 | tf_op jit(solution)/shard_map/ppermute | solution.py:301
  18.6 6.9 %collective-permute-start.3 = (bf16[256,256]{1,0:T(8,128)(2,1)S(1)}, bf16[256,256]{1,0:T(8,128)(2,1)S(1)}, u32[]{:S(2)}, u32[]{:S(2)}) collective-permute-start(bf16[256,256]{1,0:T(8,128)(2,1)S(1)} %collective-permute-done.1.refs_1_), channel_id=1, source_target_pairs={{0,4},{4,0},{8,12},{12,8},{16,20},{20,16},{24,28},{28,24},{1,5},{5... | collective-permute-start | bytes 393224 | tf_op jit(solution)/shard_map/ppermute | solution.py:301
  29.8 2.0 %collective-permute-start.7 = (bf16[64,4096]{1,0:T(8,128)(2,1)S(1)}, bf16[64,4096]{1,0:T(8,128)(2,1)S(1)}, u32[]{:S(2)}, u32[]{:S(2)}) collective-permute-start(bf16[64,4096]{1,0:T(8,128)(2,1)S(1)} %get-tuple-element.24), channel_id=1, source_target_pairs={{0,1},{1,0},{2,3},{3,2},{4,5},{5,4},{6,7},{7,6},{8,9},{9,8},{10,11... | collective-permute-start | bytes 1572872 | tf_op jit(solution)/shard_map/ppermute | solution.py:340
  31.8 8.4 %collective-permute-start.8 = (bf16[32,4096]{1,0:T(8,128)(2,1)S(1)}, bf16[32,4096]{1,0:T(8,128)(2,1)S(1)}, u32[]{:S(2)}, u32[]{:S(2)}) collective-permute-start(bf16[32,4096]{1,0:T(8,128)(2,1)S(1)} %add_convert_fusion.1), channel_id=1, source_target_pairs={{0,2},{1,3},{2,0},{3,1},{4,6},{5,7},{6,4},{7,5},{8,10},{9,11},{10,... | collective-permute-start | bytes 786440 | tf_op jit(solution)/shard_map/ppermute | solution.py:343

commit v3 on v2

--- a/solution.py
+++ b/solution.py
@@ -232,8 +232,28 @@
     wait_all(loads)
 
 
+def again(slots, seen_ref, qr_ref, top_in, sum_in, *refs):
+    kv_refs, (top_ref, sum_ref, kv_ref, seen_smem, sem) = refs[: len(slots)], refs[len(slots) :]
+    seen_blocks(slots, seen_ref, seen_smem, sem, qr_ref, top_ref, sum_ref, kv_refs, kv_ref)
+
+
+def project(att_ref, w_refs, first, chunk, give_ref, keep_ref):
+    half = att_ref.shape[0] // 2
+    for j in range(give_ref.shape[1] // chunk):
+        product, depth = None, 0
+        for w_ref in w_refs:
+            term = jnp.dot(
+                att_ref[:, depth : depth + w_ref.shape[0]],
+                w_ref[:, first + j * chunk : first + (j + 1) * chunk],
+                preferred_element_type=jnp.float32)
+            product = term if product is None else product + term
+            depth += w_ref.shape[0]
+        give_ref[:, j * chunk : (j + 1) * chunk] = product[:half].astype(jnp.bfloat16)
+        keep_ref[:, j * chunk : (j + 1) * chunk] = product[half:]
+
+
 def finish(slots, chunk, seen_ref, qr_ref, top_in, sum_in, *refs):
-    kv_refs, (w0_ref, w1_ref, top_ref, sum_ref, give_ref, keep_ref, att_ref, kv_ref, seen_smem, sem) = (
+    kv_refs, (w0_ref, w1_ref, top_ref, sum_ref, att_ref, give_ref, keep_ref, kv_ref, seen_smem, sem) = (
         refs[: len(slots)], refs[len(slots) :])
     seen_blocks(slots, seen_ref, seen_smem, sem, qr_ref, top_ref, sum_ref, kv_refs, kv_ref)
     rows, width = att_ref.shape
@@ -242,13 +262,11 @@
         att_ref[:, h * HEAD_SIZE : (h + 1) * HEAD_SIZE] = (
             sum_ref[at, :HEAD_SIZE] / sum_ref[at, HEAD_SIZE:]
         ).astype(jnp.bfloat16)
-    depth = w0_ref.shape[0]
-    for j in range(w0_ref.shape[1] // chunk):
-        cols = slice(j * chunk, (j + 1) * chunk)
-        product = jnp.dot(att_ref[:, :depth], w0_ref[:, cols], preferred_element_type=jnp.float32)
-        product += jnp.dot(att_ref[:, depth:], w1_ref[:, cols], preferred_element_type=jnp.float32)
-        give_ref[:, cols] = product[: rows // 2].astype(jnp.bfloat16)
-        keep_ref[:, cols] = product[rows // 2 :]
+    project(att_ref, (w0_ref, w1_ref), 0, chunk, give_ref, keep_ref)
+
+
+def rest(chunk, att_ref, w0_ref, w1_ref, give_ref, keep_ref):
+    project(att_ref, (w0_ref, w1_ref), w0_ref.shape[1] - give_ref.shape[1], chunk, give_ref, keep_ref)
 
 
 def in_hbm(x):
@@ -329,19 +347,34 @@
         + [("vmem", x) for x in (qr, top, sums, *(got[s] for s in slots))],
         states + [half_weight], [held(slots)] + small + [dma((8,))],
         flops=4 * 10**9, aliases={3: 0, 4: 1}, limit=8)
-    slots = (3, 7, 6, 5)
-    _, _, give, keep = kernel(
-        functools.partial(finish, slots, 512),
+    slots = (3, 7)
+    top, sums = kernel(
+        functools.partial(again, slots),
+        [("vmem", x) for x in (seen, qr, top, sums, *(got[s] for s in slots))],
+        states, [held(slots)] + small, flops=10**9, aliases={2: 0, 3: 1}, limit=8)
+    slots = (6, 5)
+    part, chunk, half = rows // n_tp, 512, out_width // 2
+    shares = [((rows // 2, half), bf16), ((rows // 2, half), f32)]
+    _, _, att, give0, keep0 = kernel(
+        functools.partial(finish, slots, chunk),
         [("vmem", x) for x in (seen, qr, top, sums, *(got[s] for s in slots), weight0, weight1)],
-        states + [((rows // 2, out_width), bf16), ((rows // 2, out_width), f32)],
-        [pltpu.VMEM((rows, width), bf16), held(slots)] + small,
-        flops=2 * rows * width * out_width, aliases={2: 0, 3: 1}, limit=8)
-    part = rows // n_tp
-    got = lax.ppermute(give, "tp", [(i, i ^ 1) for i in range(n_tp)])
-    far = (keep[:part] + got[:part].astype(f32)).astype(bf16)
-    near = keep[part:] + got[part:].astype(f32)
-    crossed = lax.ppermute(far, "tp", [(i, i ^ 2) for i in range(n_tp)])
-    return (near + crossed.astype(f32)).astype(bf16)
+        states + [((rows, width), bf16)] + shares, [held(slots)] + small,
+        flops=rows * width * out_width, aliases={2: 0, 3: 1}, limit=8)
+
+    def across(x, hop):
+        return lax.ppermute(x, "tp", [(i, i ^ hop) for i in range(n_tp)])
+
+    got0 = across(give0, 1)
+    give1, keep1 = kernel(
+        functools.partial(rest, chunk), [("vmem", x) for x in (att, weight0, weight1)],
+        shares, flops=rows * width * out_width, limit=8)
+    got1 = across(give1, 1)
+    ends = []
+    for keep, other in ((keep0, got0), (keep1, got1)):
+        far = (keep[:part] + other[:part].astype(f32)).astype(bf16)
+        crossed = across(far, 2)
+        ends.append((keep[part:] + other[part:].astype(f32) + crossed.astype(f32)).astype(bf16))
+    return jnp.concatenate(ends, 1)
 
 
 def solution(mesh):

time: 41.2 us -> 41.6 us (level)
  waiting for transfers between devices: 16 us -> 14.5 us
  starting transfers between devices: 11 us -> 12 us
  Pallas kernels: 13.2 us -> 13.9 us
    ppermute x2 -> x4, waiting for transfers between devices: 8.72 us -> 7.2 us  [across(): return lax.ppermute(x, 'tp', [(i, i ^ hop) for i in range(n_tp)])]
    ppermute x2 -> x4, starting transfers between devices: 1.66 us -> 2.72 us  [across(): return lax.ppermute(x, 'tp', [(i, i ^ hop) for i in range(n_tp)])]
    pallas_call x4 -> x6, Pallas kernels: 13.2 us -> 13.9 us  [kernel(): pl.pallas_call(body, out_shape=tuple((pltpu.VMEM(shape, dtype) for shape,...]
    concatenate x0 -> x1, other arithmetic: none -> 0.72 us  [blockwise(): return jnp.concatenate(ends, 1)]
    convert_element_type x2 -> x4, other arithmetic: 0.83 us -> 0.14 us  [the longest x2 0.09 us: blockwise(): (keep[part:] + other[part:].astype(f32) + crossed.astype(f32)).astype(bf16)]
  transfers between devices with their start and end apart: 9 -> 11, of which waited for: 5 -> 5; matrix products, arithmetic and copies ran while one was open for 0% -> 0% of each run, Pallas kernels for 19% -> 24%
where the time goes in v3:
time: 41.6 us; the launch traced here: 41.4 us
  waiting for transfers between devices  14.5 us (35%)
  Pallas kernels  13.9 us (33%)
  starting transfers between devices  12 us (29%)
  other arithmetic  0.86 us (2%)
    pallas_call x6, Pallas kernels, kernel(): pl.pallas_call(body, out_shape=tuple((pltpu.VMEM(shape, dtype) for shape,...  13.9 us
    ppermute x7, starting transfers between devices, swap(): return lax.ppermute(block, 'cp', [(i, i ^ s) for i in range(n)])  9.31 us
    ppermute x7, waiting for transfers between devices, swap(): return lax.ppermute(block, 'cp', [(i, i ^ s) for i in range(n)])  7.29 us
    ppermute x4, waiting for transfers between devices, across(): return lax.ppermute(x, 'tp', [(i, i ^ hop) for i in range(n_tp)])  7.2 us
    ppermute x4, starting transfers between devices, across(): return lax.ppermute(x, 'tp', [(i, i ^ hop) for i in range(n_tp)])  2.72 us
  transfers between devices with their start and end apart: 11, of which 5 were waited for; matrix products, arithmetic and copies ran while one was open for 0% of the time, Pallas kernels for 24%

profile of v3, /device:TPU:0, one launch (start us, length us, event | category | flops | bytes accessed | tf_op | source)
XLA Modules:
  0.0 41.4 jit_solution(12279962112575013682)
XLA Ops:
  0.0 0.9 %shard_map.64.kv_ref = bf16[256,256]{1,0:T(8,128)(2,1)S(1)} custom-call(bf16[128,256]{1,0:T(8,128)(2,1)} %k_hbm.1, bf16[128,256]{1,0:T(8,128)(2,1)} %v_hbm.1), custom_call_target="tpu_custom_call" | custom-call | tf_op jit(solution)/shard_map/pallas_call | solution.py:285
  0.9 6.1 %collective-permute-start.4 = (bf16[256,256]{1,0:T(8,128)(2,1)S(1)}, bf16[256,256]{1,0:T(8,128)(2,1)S(1)}, u32[]{:S(2)}, u32[]{:S(2)}) collective-permute-start(bf16[256,256]{1,0:T(8,128)(2,1)S(1)} %shard_map.64.kv_ref), channel_id=1, source_target_pairs={{0,28},{4,24},{8,20},{12,16},{16,12},{20,8},{24,4},{28,0},{1,29},{... | collective-permute-start | bytes 393224 | tf_op jit(solution)/shard_map/ppermute | solution.py:319
  7.0 0.0 collective-permute-start.2
  7.0 0.8 %collective-permute-start.1 = (bf16[256,256]{1,0:T(8,128)(2,1)S(1)}, bf16[256,256]{1,0:T(8,128)(2,1)S(1)}, u32[]{:S(2)}, u32[]{:S(2)}) collective-permute-start(bf16[256,256]{1,0:T(8,128)(2,1)S(1)} %shard_map.64.kv_ref), channel_id=1, source_target_pairs={{0,8},{4,12},{8,0},{12,4},{16,24},{20,28},{24,16},{28,20},{1,9},{5... | collective-permute-start | bytes 393224 | tf_op jit(solution)/shard_map/ppermute | solution.py:319
  7.8 0.4 %collective-permute-start = (bf16[256,256]{1,0:T(8,128)(2,1)S(1)}, bf16[256,256]{1,0:T(8,128)(2,1)S(1)}, u32[]{:S(2)}, u32[]{:S(2)}) collective-permute-start(bf16[256,256]{1,0:T(8,128)(2,1)S(1)} %shard_map.64.kv_ref), channel_id=1, source_target_pairs={{0,4},{4,0},{8,12},{12,8},{16,20},{20,16},{24,28},{28,24},{1,5},{5... | collective-permute-start | bytes 393224 | tf_op jit(solution)/shard_map/ppermute | solution.py:319
  8.2 4.5 %shard_map.65 = (bf16[2048,128]{1,0:T(8,128)(2,1)S(1)}, s32[8,128]{1,0:T(8,128)S(1)}, f32[2048,128]{1,0:T(8,128)S(1)}, f32[2048,256]{1,0:T(8,128)S(1)}, bf16[1024,4096]{1,0:T(8,128)(2,1)S(1)}) custom-call(s32[8]{0:T(128)} %order_hbm.1, s32[4]{0:T(128)} %docs_hbm.1, bf16[128,2048]{1,0:T(8,128)(2,1)} %q_hbm.1, bf16[2048,4096]{1,0:T(8,128)(2,1)} %w_hbm.3, ...), custom_call_target="tpu_custom_call" | custom-call | flops 4000000000 | tf_op jit(solution)/shard_map/pallas_call | solution.py:285
  12.7 5.4 %collective-permute-done.2.refs_2_ = bf16[256,256]{1,0:T(8,128)(2,1)S(1)} collective-permute-done((bf16[256,256]{1,0:T(8,128)(2,1)S(1)}, bf16[256,256]{1,0:T(8,128)(2,1)S(1)}, u32[]{:S(2)}, u32[]{:S(2)}) %collective-permute-start.2) | collective-permute-done | bytes 131104 | tf_op jit(solution)/shard_map/ppermute | solution.py:319
  18.0 0.5 %collective-permute-start.6 = (bf16[256,256]{1,0:T(8,128)(2,1)S(1)}, bf16[256,256]{1,0:T(8,128)(2,1)S(1)}, u32[]{:S(2)}, u32[]{:S(2)}) collective-permute-start(bf16[256,256]{1,0:T(8,128)(2,1)S(1)} %collective-permute-done.2.refs_2_), channel_id=1, source_target_pairs={{0,4},{4,0},{8,12},{12,8},{16,20},{20,16},{24,28},{28,24},{1,5},{5... | collective-permute-start | bytes 393224 | tf_op jit(solution)/shard_map/ppermute | solution.py:319
  18.6 0.0 collective-permute-start.5
  18.6 0.0 collective-permute-done.1.refs_1_
  18.6 1.5 %collective-permute-start.3 = (bf16[256,256]{1,0:T(8,128)(2,1)S(1)}, bf16[256,256]{1,0:T(8,128)(2,1)S(1)}, u32[]{:S(2)}, u32[]{:S(2)}) collective-permute-start(bf16[256,256]{1,0:T(8,128)(2,1)S(1)} %collective-permute-done.1.refs_1_), channel_id=1, source_target_pairs={{0,4},{4,0},{8,12},{12,8},{16,20},{20,16},{24,28},{28,24},{1,5},{5... | collective-permute-start | bytes 393224 | tf_op jit(solution)/shard_map/ppermute | solution.py:319
  20.1 0.0 collective-permute-done.refs_0_
  20.1 3.5 %shard_map.66 = (f32[2048,128]{1,0:T(8,128)S(1)}, f32[2048,256]{1,0:T(8,128)S(1)}, bf16[1024,4096]{1,0:T(8,128)(2,1)S(1)}) custom-call(s32[8,128]{1,0:T(8,128)S(1)} %get-tuple-element.20.seen_ref, bf16[2048,4096]{1,0:T(8,128)(2,1)} %w_hbm.3, bf16[2048,128]{1,0:T(8,128)(2,1)S(1)} %get-tuple-element.21.qr_ref, ...), custom_call_target="tpu_custom_call", output_to_operand_aliasing={{0}: (3, {}), {1}: (4, {})} | custom-call | flops 4000000000 | tf_op jit(solution)/shard_map/pallas_call | solution.py:285
  23.6 0.0 collective-permute-done.4.refs_1_
  23.6 1.9 %collective-permute-done.3.refs_0_ = bf16[256,256]{1,0:T(8,128)(2,1)S(1)} collective-permute-done((bf16[256,256]{1,0:T(8,128)(2,1)S(1)}, bf16[256,256]{1,0:T(8,128)(2,1)S(1)}, u32[]{:S(2)}, u32[]{:S(2)}) %collective-permute-start.3) | collective-permute-done | bytes 131104 | tf_op jit(solution)/shard_map/ppermute | solution.py:319
  25.5 1.8 %shard_map.67 = (f32[2048,128]{1,0:T(8,128)S(1)}, f32[2048,256]{1,0:T(8,128)S(1)}) custom-call(s32[8,128]{1,0:T(8,128)S(1)} %get-tuple-element.20.seen_ref, bf16[2048,128]{1,0:T(8,128)(2,1)S(1)} %get-tuple-element.21.qr_ref, f32[2048,128]{1,0:T(8,128)S(1)} %get-tuple-element.24.top_in, ...), custom_call_target="tpu_custom_call", output_to_operand_aliasing={{0}: (2, {}), {1}: (3, {})} | custom-call | flops 1000000000 | tf_op jit(solution)/shard_map/pallas_call | solution.py:285
  27.3 0.0 collective-permute-done.6.refs_1_
  27.3 0.0 collective-permute-done.5.refs_0_
  27.3 2.0 %shard_map.68 = (f32[2048,128]{1,0:T(8,128)S(1)}, f32[2048,256]{1,0:T(8,128)S(1)}, bf16[128,2048]{1,0:T(8,128)(2,1)S(1)}, bf16[64,2048]{1,0:T(8,128)(2,1)S(1)}, f32[64,2048]{1,0:T(8,128)S(1)}) custom-call(s32[8,128]{1,0:T(8,128)S(1)} %get-tuple-element.20.seen_ref, ...), custom_call_target="tpu_custom_call", output_to_operand_aliasing={{0}: (2, {}), {1}: (3, {})} | custom-call | flops 1073741824 | tf_op jit(solution)/shard_map/pallas_call | solution.py:285
  29.3 1.3 %shard_map.69 = (bf16[64,2048]{1,0:T(8,128)(2,1)S(1)}, f32[64,2048]{1,0:T(8,128)S(1)}) custom-call(bf16[128,2048]{1,0:T(8,128)(2,1)S(1)} %get-tuple-element.32.att_ref, bf16[1024,4096]{1,0:T(8,128)(2,1)S(1)} %get-tuple-element.28.refs_2_.w0_ref, bf16[1024,4096]{1,0:T(8,128)(2,1)S(1)} %get-tuple-element.29.refs_3_.w1_ref), custom_call_target="tpu_custom_call" | custom-call | flops 1073741824 | tf_op jit(solution)/shard_map/pallas_call | solution.py:285
  30.6 0.1 collective-permute-start.9
  30.7 0.5 %collective-permute-start.7 = (bf16[64,2048]{1,0:T(8,128)(2,1)S(1)}, bf16[64,2048]{1,0:T(8,128)(2,1)S(1)}, u32[]{:S(2)}, u32[]{:S(2)}) collective-permute-start(bf16[64,2048]{1,0:T(8,128)(2,1)S(1)} %get-tuple-element.31), channel_id=1, source_target_pairs={{0,1},{1,0},{2,3},{3,2},{4,5},{5,4},{6,7},{7,6},{8,9},{9,8},{10,11... | collective-permute-start | bytes 786440 | tf_op jit(solution)/shard_map/ppermute | solution.py:365
  31.2 1.0 %collective-permute-done.9 = bf16[64,2048]{1,0:T(8,128)(2,1)S(1)} collective-permute-done((bf16[64,2048]{1,0:T(8,128)(2,1)S(1)}, bf16[64,2048]{1,0:T(8,128)(2,1)S(1)}, u32[]{:S(2)}, u32[]{:S(2)}) %collective-permute-start.9) | collective-permute-done | bytes 262176 | tf_op jit(solution)/shard_map/ppermute | solution.py:365
  32.2 1.6 %collective-permute-start.10 = (bf16[32,2048]{1,0:T(8,128)(2,1)S(1)}, bf16[32,2048]{1,0:T(8,128)(2,1)S(1)}, u32[]{:S(2)}, u32[]{:S(2)}) collective-permute-start(bf16[32,2048]{1,0:T(8,128)(2,1)S(1)} %add_convert_fusion.1), channel_id=1, source_target_pairs={{0,2},{1,3},{2,0},{3,1},{4,6},{5,7},{6,4},{7,5},{8,10},{9,11},{10,... | collective-permute-start | bytes 393224 | tf_op jit(solution)/shard_map/ppermute | solution.py:365
  33.8 0.0 collective-permute-done.7
  33.9 0.6 %collective-permute-start.8 = (bf16[32,2048]{1,0:T(8,128)(2,1)S(1)}, bf16[32,2048]{1,0:T(8,128)(2,1)S(1)}, u32[]{:S(2)}, u32[]{:S(2)}) collective-permute-start(bf16[32,2048]{1,0:T(8,128)(2,1)S(1)} %add_convert_fusion.3), channel_id=1, source_target_pairs={{0,2},{1,3},{2,0},{3,1},{4,6},{5,7},{6,4},{7,5},{8,10},{9,11},{10,... | collective-permute-start | bytes 393224 | tf_op jit(solution)/shard_map/ppermute | solution.py:365
  34.4 4.2 %collective-permute-done.10 = bf16[32,2048]{1,0:T(8,128)(2,1)S(1)} collective-permute-done((bf16[32,2048]{1,0:T(8,128)(2,1)S(1)}, bf16[32,2048]{1,0:T(8,128)(2,1)S(1)}, u32[]{:S(2)}, u32[]{:S(2)}) %collective-permute-start.10) | collective-permute-done | bytes 131104 | tf_op jit(solution)/shard_map/ppermute | solution.py:365
  38.7 1.9 %collective-permute-done.8 = bf16[32,2048]{1,0:T(8,128)(2,1)S(1)} collective-permute-done((bf16[32,2048]{1,0:T(8,128)(2,1)S(1)}, bf16[32,2048]{1,0:T(8,128)(2,1)S(1)}, u32[]{:S(2)}, u32[]{:S(2)}) %collective-permute-start.8) | collective-permute-done | bytes 131104 | tf_op jit(solution)/shard_map/ppermute | solution.py:365
  40.7 0.7 %pad_maximum_fusion = bf16[32,4096]{1,0:T(8,128)(2,1)} fusion(bf16[32,2048]{1,0:T(8,128)(2,1)S(1)} %add_convert_fusion, bf16[32,2048]{1,0:T(8,128)(2,1)S(1)} %add_convert_fusion.2), kind=kLoop, calls=%fused_computation | loop fusion | flops 524288 | bytes 524288 | tf_op jit(solution)/shard_map/concatenate | solution.py:377
  (4 shorter events, 0.1 us)
Async XLA Ops:
  0.9 22.7 %collective-permute-start.4 = (bf16[256,256]{1,0:T(8,128)(2,1)S(1)}, bf16[256,256]{1,0:T(8,128)(2,1)S(1)}, u32[]{:S(2)}, u32[]{:S(2)}) collective-permute-start(bf16[256,256]{1,0:T(8,128)(2,1)S(1)} %shard_map.64.kv_ref), channel_id=1, source_target_pairs={{0,28},{4,24},{8,20},{12,16},{16,12},{20,8},{24,4},{28,0},{1,29},{... | collective-permute-start | bytes 393224 | tf_op jit(solution)/shard_map/ppermute | solution.py:319
  7.0 11.1 %collective-permute-start.2 = (bf16[256,256]{1,0:T(8,128)(2,1)S(1)}, bf16[256,256]{1,0:T(8,128)(2,1)S(1)}, u32[]{:S(2)}, u32[]{:S(2)}) collective-permute-start(bf16[256,256]{1,0:T(8,128)(2,1)S(1)} %shard_map.64.kv_ref), channel_id=1, source_target_pairs={{0,16},{4,20},{8,24},{12,28},{16,0},{20,4},{24,8},{28,12},{1,17},{... | collective-permute-start | bytes 393224 | tf_op jit(solution)/shard_map/ppermute | solution.py:319
  7.0 11.6 %collective-permute-start.1 = (bf16[256,256]{1,0:T(8,128)(2,1)S(1)}, bf16[256,256]{1,0:T(8,128)(2,1)S(1)}, u32[]{:S(2)}, u32[]{:S(2)}) collective-permute-start(bf16[256,256]{1,0:T(8,128)(2,1)S(1)} %shard_map.64.kv_ref), channel_id=1, source_target_pairs={{0,8},{4,12},{8,0},{12,4},{16,24},{20,28},{24,16},{28,20},{1,9},{5... | collective-permute-start | bytes 393224 | tf_op jit(solution)/shard_map/ppermute | solution.py:319
  7.8 12.3 %collective-permute-start = (bf16[256,256]{1,0:T(8,128)(2,1)S(1)}, bf16[256,256]{1,0:T(8,128)(2,1)S(1)}, u32[]{:S(2)}, u32[]{:S(2)}) collective-permute-start(bf16[256,256]{1,0:T(8,128)(2,1)S(1)} %shard_map.64.kv_ref), channel_id=1, source_target_pairs={{0,4},{4,0},{8,12},{12,8},{16,20},{20,16},{24,28},{28,24},{1,5},{5... | collective-permute-start | bytes 393224 | tf_op jit(solution)/shard_map/ppermute | solution.py:319
  18.0 9.3 %collective-permute-start.6 = (bf16[256,256]{1,0:T(8,128)(2,1)S(1)}, bf16[256,256]{1,0:T(8,128)(2,1)S(1)}, u32[]{:S(2)}, u32[]{:S(2)}) collective-permute-start(bf16[256,256]{1,0:T(8,128)(2,1)S(1)} %collective-permute-done.2.refs_2_), channel_id=1, source_target_pairs={{0,4},{4,0},{8,12},{12,8},{16,20},{20,16},{24,28},{28,24},{1,5},{5... | collective-permute-start | bytes 393224 | tf_op jit(solution)/shard_map/ppermute | solution.py:319
  18.6 8.7 %collective-permute-start.5 = (bf16[256,256]{1,0:T(8,128)(2,1)S(1)}, bf16[256,256]{1,0:T(8,128)(2,1)S(1)}, u32[]{:S(2)}, u32[]{:S(2)}) collective-permute-start(bf16[256,256]{1,0:T(8,128)(2,1)S(1)} %collective-permute-done.2.refs_2_), channel_id=1, source_target_pairs={{0,8},{4,12},{8,0},{12,4},{16,24},{20,28},{24,16},{28,20},{1,9},{5... | collective-permute-start | bytes 393224 | tf_op jit(solution)/shard_map/ppermute | solution.py:319
  18.6 6.9 %collective-permute-start.3 = (bf16[256,256]{1,0:T(8,128)(2,1)S(1)}, bf16[256,256]{1,0:T(8,128)(2,1)S(1)}, u32[]{:S(2)}, u32[]{:S(2)}) collective-permute-start(bf16[256,256]{1,0:T(8,128)(2,1)S(1)} %collective-permute-done.1.refs_1_), channel_id=1, source_target_pairs={{0,4},{4,0},{8,12},{12,8},{16,20},{20,16},{24,28},{28,24},{1,5},{5... | collective-permute-start | bytes 393224 | tf_op jit(solution)/shard_map/ppermute | solution.py:319
  30.6 1.6 %collective-permute-start.9 = (bf16[64,2048]{1,0:T(8,128)(2,1)S(1)}, bf16[64,2048]{1,0:T(8,128)(2,1)S(1)}, u32[]{:S(2)}, u32[]{:S(2)}) collective-permute-start(bf16[64,2048]{1,0:T(8,128)(2,1)S(1)} %get-tuple-element.34), channel_id=1, source_target_pairs={{0,1},{1,0},{2,3},{3,2},{4,5},{5,4},{6,7},{7,6},{8,9},{9,8},{10,11... | collective-permute-start | bytes 786440 | tf_op jit(solution)/shard_map/ppermute | solution.py:365
  30.7 3.1 %collective-permute-start.7 = (bf16[64,2048]{1,0:T(8,128)(2,1)S(1)}, bf16[64,2048]{1,0:T(8,128)(2,1)S(1)}, u32[]{:S(2)}, u32[]{:S(2)}) collective-permute-start(bf16[64,2048]{1,0:T(8,128)(2,1)S(1)} %get-tuple-element.31), channel_id=1, source_target_pairs={{0,1},{1,0},{2,3},{3,2},{4,5},{5,4},{6,7},{7,6},{8,9},{9,8},{10,11... | collective-permute-start | bytes 786440 | tf_op jit(solution)/shard_map/ppermute | solution.py:365
  32.2 6.4 %collective-permute-start.10 = (bf16[32,2048]{1,0:T(8,128)(2,1)S(1)}, bf16[32,2048]{1,0:T(8,128)(2,1)S(1)}, u32[]{:S(2)}, u32[]{:S(2)}) collective-permute-start(bf16[32,2048]{1,0:T(8,128)(2,1)S(1)} %add_convert_fusion.1), channel_id=1, source_target_pairs={{0,2},{1,3},{2,0},{3,1},{4,6},{5,7},{6,4},{7,5},{8,10},{9,11},{10,... | collective-permute-start | bytes 393224 | tf_op jit(solution)/shard_map/ppermute | solution.py:365
  33.9 6.8 %collective-permute-start.8 = (bf16[32,2048]{1,0:T(8,128)(2,1)S(1)}, bf16[32,2048]{1,0:T(8,128)(2,1)S(1)}, u32[]{:S(2)}, u32[]{:S(2)}) collective-permute-start(bf16[32,2048]{1,0:T(8,128)(2,1)S(1)} %add_convert_fusion.3), channel_id=1, source_target_pairs={{0,2},{1,3},{2,0},{3,1},{4,6},{5,7},{6,4},{7,5},{8,10},{9,11},{10,... | collective-permute-start | bytes 393224 | tf_op jit(solution)/shard_map/ppermute | solution.py:365

commit v4 on v3

--- a/solution.py
+++ b/solution.py
@@ -127,7 +127,7 @@
     sum_ref[at, :] = sums
 
 
-def sweep(qr_ref, top_ref, sum_ref, kvs, bias, fresh=False, pieces=2):
+def sweep(qr_ref, top_ref, sum_ref, kvs, bias, fresh=False):
     heads_kv = kvs[0].shape[1] // HEAD_SIZE
     height = qr_ref.shape[0] // heads_kv
     for g in range(heads_kv):
@@ -135,9 +135,8 @@
         key_rows = jnp.concatenate([ref[:BLOCK_TOKENS, cols] for ref in kvs], 0)
         value_rows = jnp.concatenate([ref[BLOCK_TOKENS:, cols] for ref in kvs], 0)
         value_rows = jnp.concatenate([value_rows, jnp.ones_like(value_rows)], 1)
-        for i in range(pieces):
-            at = pl.ds(g * height + i * (height // pieces), height // pieces)
-            online(top_ref, sum_ref, at, qr_ref[at, :], key_rows, value_rows, bias, fresh)
+        at = pl.ds(g * height, height)
+        online(top_ref, sum_ref, at, qr_ref[at, :], key_rows, value_rows, bias, fresh)
 
 
 def start_all(copies):
@@ -199,15 +198,14 @@
     bias = jnp.concatenate(
         [jnp.where(key_at <= row_at + target * part, 0.0, MASKED) for target in targets], 0)
     heads = width // kv_ref.shape[1]
-    sweep(qr_ref, top_ref, sum_ref, [kv_ref], jnp.concatenate([bias] * (heads // 2), 0), fresh=True)
+    sweep(qr_ref, top_ref, sum_ref, [kv_ref], jnp.concatenate([bias] * heads, 0), fresh=True)
     wait_all(loads)
 
 
-def seen_blocks(slots, seen_hbm, seen_smem, sem, qr_ref, top_ref, sum_ref, kv_refs, kv_ref):
-    wait_all(start_all([pltpu.make_async_copy(seen_hbm, seen_smem, sem)]))
+def seen_blocks(slots, seen_ref, qr_ref, top_ref, sum_ref, kv_refs, kv_ref):
     used = jnp.int32(0)
     for s, ref in zip(slots, kv_refs):
-        wanted = seen_smem[s, 0]
+        wanted = jnp.max(seen_ref[s : s + 1, :])
 
         @pl.when(wanted == 1)
         def _(ref=ref, used=used):
@@ -218,6 +216,7 @@
         for count in (1, 2):
             if first + count > kv_ref.shape[0]:
                 continue
+            last = first + count == kv_ref.shape[0]
 
             @pl.when((used >= first + 2) if count == 2 else (used == first + 1))
             def _(first=first, count=count):
@@ -225,16 +224,16 @@
 
 
 def more(slots, seen_ref, w_hbm, qr_ref, top_in, sum_in, *refs):
-    kv_refs, (top_ref, sum_ref, w_ref, kv_ref, seen_smem, sem, w_sems) = (
+    kv_refs, (top_ref, sum_ref, w_ref, kv_ref, w_sems) = (
         refs[: len(slots)], refs[len(slots) :])
     loads = load_rows(w_hbm, w_ref.shape[0], w_ref, w_sems)
-    seen_blocks(slots, seen_ref, seen_smem, sem, qr_ref, top_ref, sum_ref, kv_refs, kv_ref)
+    seen_blocks(slots, seen_ref, qr_ref, top_ref, sum_ref, kv_refs, kv_ref)
     wait_all(loads)
 
 
 def again(slots, seen_ref, qr_ref, top_in, sum_in, *refs):
-    kv_refs, (top_ref, sum_ref, kv_ref, seen_smem, sem) = refs[: len(slots)], refs[len(slots) :]
-    seen_blocks(slots, seen_ref, seen_smem, sem, qr_ref, top_ref, sum_ref, kv_refs, kv_ref)
+    kv_refs, (top_ref, sum_ref, kv_ref) = refs[: len(slots)], refs[len(slots) :]
+    seen_blocks(slots, seen_ref, qr_ref, top_ref, sum_ref, kv_refs, kv_ref)
 
 
 def project(att_ref, w_refs, first, chunk, give_ref, keep_ref):
@@ -253,20 +252,29 @@
 
 
 def finish(slots, chunk, seen_ref, qr_ref, top_in, sum_in, *refs):
-    kv_refs, (w0_ref, w1_ref, top_ref, sum_ref, att_ref, give_ref, keep_ref, kv_ref, seen_smem, sem) = (
+    kv_refs, (w0_ref, w1_ref, top_ref, sum_ref, att_ref, give_ref, keep_ref, kv_ref) = (
         refs[: len(slots)], refs[len(slots) :])
-    seen_blocks(slots, seen_ref, seen_smem, sem, qr_ref, top_ref, sum_ref, kv_refs, kv_ref)
+    seen_blocks(slots, seen_ref, qr_ref, top_ref, sum_ref, kv_refs, kv_ref)
     rows, width = att_ref.shape
     for h in range(width // HEAD_SIZE):
         at = slice(h * rows, (h + 1) * rows)
         att_ref[:, h * HEAD_SIZE : (h + 1) * HEAD_SIZE] = (
-            sum_ref[at, :HEAD_SIZE] / sum_ref[at, HEAD_SIZE:]
+            sum_ref[at, :HEAD_SIZE] * pl.reciprocal(sum_ref[at, HEAD_SIZE:])
         ).astype(jnp.bfloat16)
     project(att_ref, (w0_ref, w1_ref), 0, chunk, give_ref, keep_ref)
 
 
 def rest(chunk, att_ref, w0_ref, w1_ref, give_ref, keep_ref):
     project(att_ref, (w0_ref, w1_ref), w0_ref.shape[1] - give_ref.shape[1], chunk, give_ref, keep_ref)
+
+
+def last(at, keep_ref, other_ref, crossed_ref, *refs):
+    out_hbm, out_ref, sem = refs[-3:]
+    part, width = out_ref.shape
+    out_ref[...] = (
+        keep_ref[part:] + other_ref[part:].astype(jnp.float32) + crossed_ref[...].astype(jnp.float32)
+    ).astype(out_ref.dtype)
+    wait_all(start_all([pltpu.make_async_copy(out_ref, out_hbm.at[:, pl.ds(at, width)], sem)]))
 
 
 def in_hbm(x):
@@ -335,7 +343,6 @@
         [pltpu.VMEM((rows, width), bf16), pltpu.SMEM(block_order.shape, jnp.int32),
          pltpu.SMEM(doc_blocks.shape, jnp.int32), dma((3,)), dma((8,))],
         flops=4 * 10**9, limit=8)
-    small = [pltpu.SMEM((n, HEAD_SIZE), jnp.int32), dma(())]
 
     def held(slots):
         return pltpu.VMEM((min(len(slots), n // 2 - 1),) + kv.shape, bf16)
@@ -345,20 +352,20 @@
         functools.partial(more, slots),
         [("vmem", seen), ("hbm", out_weight)]
         + [("vmem", x) for x in (qr, top, sums, *(got[s] for s in slots))],
-        states + [half_weight], [held(slots)] + small + [dma((8,))],
+        states + [half_weight], [held(slots), dma((8,))],
         flops=4 * 10**9, aliases={3: 0, 4: 1}, limit=8)
-    slots = (3, 7)
+    slots = (3, 7, 6)
     top, sums = kernel(
         functools.partial(again, slots),
         [("vmem", x) for x in (seen, qr, top, sums, *(got[s] for s in slots))],
-        states, [held(slots)] + small, flops=10**9, aliases={2: 0, 3: 1}, limit=8)
-    slots = (6, 5)
+        states, [held(slots)], flops=10**9, aliases={2: 0, 3: 1}, limit=8)
+    slots = (5,)
     part, chunk, half = rows // n_tp, 512, out_width // 2
     shares = [((rows // 2, half), bf16), ((rows // 2, half), f32)]
     _, _, att, give0, keep0 = kernel(
         functools.partial(finish, slots, chunk),
         [("vmem", x) for x in (seen, qr, top, sums, *(got[s] for s in slots), weight0, weight1)],
-        states + [((rows, width), bf16)] + shares, [held(slots)] + small,
+        states + [((rows, width), bf16)] + shares, [held(slots)],
         flops=rows * width * out_width, aliases={2: 0, 3: 1}, limit=8)
 
     def across(x, hop):
@@ -369,12 +376,23 @@
         functools.partial(rest, chunk), [("vmem", x) for x in (att, weight0, weight1)],
         shares, flops=rows * width * out_width, limit=8)
     got1 = across(give1, 1)
-    ends = []
+    crossed = []
     for keep, other in ((keep0, got0), (keep1, got1)):
         far = (keep[:part] + other[:part].astype(f32)).astype(bf16)
-        crossed = across(far, 2)
-        ends.append((keep[part:] + other[part:].astype(f32) + crossed.astype(f32)).astype(bf16))
-    return jnp.concatenate(ends, 1)
+        crossed.append(across(far, 2))
+    ends = ((keep0, got0, crossed[0]), (keep1, got1, crossed[1]))
+    out = ()
+    for i, terms in enumerate(ends):
+        out = pl.pallas_call(
+            functools.partial(last, i * half),
+            out_shape=(pltpu.HBM((part, out_width), bf16),),
+            in_specs=[VMEM] * 3 + [HBM] * len(out),
+            out_specs=(HBM,),
+            scratch_shapes=[pltpu.VMEM((part, half), bf16), dma(())],
+            input_output_aliases={3: 0} if out else {},
+            compiler_params=pltpu.CompilerParams(vmem_limit_bytes=8 * 1024 * 1024),
+        )(*map(in_vmem, terms), *out)
+    return out[0]
 
 
 def solution(mesh):

time: 41.6 us -> 39.8 us (0.957)
  waiting for transfers between devices: 14.5 us -> 12.3 us
  other arithmetic: 0.86 us -> 0.06 us
  Pallas kernels: 13.9 us -> 14.6 us
  starting transfers between devices: 12 us -> 12.6 us
    ppermute x4, waiting for transfers between devices: 7.2 us -> 4.84 us  [across(): return lax.ppermute(x, 'tp', [(i, i ^ hop) for i in range(n_tp)])]
    pallas_call x0 -> x2, Pallas kernels: none -> 1.42 us  [blockwise(): pl.pallas_call(functools.partial(last, i * half), out_shape=(pltpu.HBM((p...]
    pallas_call x6, Pallas kernels: 13.9 us -> 13.1 us  [kernel(): pl.pallas_call(body, out_shape=tuple((pltpu.VMEM(shape, dtype) for shape,...]
    concatenate x1 -> x0, other arithmetic: 0.72 us -> none  [blockwise(): return jnp.concatenate(ends, 1)]
    ppermute x4, starting transfers between devices: 2.72 us -> 3.34 us  [across(): return lax.ppermute(x, 'tp', [(i, i ^ hop) for i in range(n_tp)])]
  transfers between devices with their start and end apart: 11 -> 11, of which waited for: 5 -> 4; matrix products, arithmetic and copies ran while one was open for 0% -> 0% of each run, Pallas kernels for 24% -> 29%
where the time goes in v4:
time: 39.8 us; the launch traced here: 39.7 us
  Pallas kernels  14.6 us (37%)
  starting transfers between devices  12.6 us (32%)
  waiting for transfers between devices  12.3 us (31%)
    pallas_call x6, Pallas kernels, kernel(): pl.pallas_call(body, out_shape=tuple((pltpu.VMEM(shape, dtype) for shape,...  13.1 us
    ppermute x7, starting transfers between devices, swap(): return lax.ppermute(block, 'cp', [(i, i ^ s) for i in range(n)])  9.31 us
    ppermute x7, waiting for transfers between devices, swap(): return lax.ppermute(block, 'cp', [(i, i ^ s) for i in range(n)])  7.47 us
    ppermute x4, waiting for transfers between devices, across(): return lax.ppermute(x, 'tp', [(i, i ^ hop) for i in range(n_tp)])  4.84 us
    ppermute x4, starting transfers between devices, across(): return lax.ppermute(x, 'tp', [(i, i ^ hop) for i in range(n_tp)])  3.34 us
    pallas_call x2, Pallas kernels, blockwise(): pl.pallas_call(functools.partial(last, i * half), out_shape=(pltpu.HBM((p...  1.42 us
  transfers between devices with their start and end apart: 11, of which 4 were waited for; matrix products, arithmetic and copies ran while one was open for 0% of the time, Pallas kernels for 29%

profile of v4, /device:TPU:0, one launch (start us, length us, event | category | flops | bytes accessed | tf_op | source)
XLA Modules:
  0.0 39.7 jit_solution(12990420731949467227)
XLA Ops:
  0.0 0.9 %shard_map.64.kv_ref = bf16[256,256]{1,0:T(8,128)(2,1)S(1)} custom-call(bf16[128,256]{1,0:T(8,128)(2,1)} %k_hbm.1, bf16[128,256]{1,0:T(8,128)(2,1)} %v_hbm.1), custom_call_target="tpu_custom_call" | custom-call | tf_op jit(solution)/shard_map/pallas_call | solution.py:293
  0.9 6.1 %collective-permute-start.4 = (bf16[256,256]{1,0:T(8,128)(2,1)S(1)}, bf16[256,256]{1,0:T(8,128)(2,1)S(1)}, u32[]{:S(2)}, u32[]{:S(2)}) collective-permute-start(bf16[256,256]{1,0:T(8,128)(2,1)S(1)} %shard_map.64.kv_ref), channel_id=1, source_target_pairs={{0,28},{4,24},{8,20},{12,16},{16,12},{20,8},{24,4},{28,0},{1,29},{... | collective-permute-start | bytes 393224 | tf_op jit(solution)/shard_map/ppermute | solution.py:327
  7.0 0.0 collective-permute-start.2
  7.0 0.8 %collective-permute-start.1 = (bf16[256,256]{1,0:T(8,128)(2,1)S(1)}, bf16[256,256]{1,0:T(8,128)(2,1)S(1)}, u32[]{:S(2)}, u32[]{:S(2)}) collective-permute-start(bf16[256,256]{1,0:T(8,128)(2,1)S(1)} %shard_map.64.kv_ref), channel_id=1, source_target_pairs={{0,8},{4,12},{8,0},{12,4},{16,24},{20,28},{24,16},{28,20},{1,9},{5... | collective-permute-start | bytes 393224 | tf_op jit(solution)/shard_map/ppermute | solution.py:327
  7.8 0.4 %collective-permute-start = (bf16[256,256]{1,0:T(8,128)(2,1)S(1)}, bf16[256,256]{1,0:T(8,128)(2,1)S(1)}, u32[]{:S(2)}, u32[]{:S(2)}) collective-permute-start(bf16[256,256]{1,0:T(8,128)(2,1)S(1)} %shard_map.64.kv_ref), channel_id=1, source_target_pairs={{0,4},{4,0},{8,12},{12,8},{16,20},{20,16},{24,28},{28,24},{1,5},{5... | collective-permute-start | bytes 393224 | tf_op jit(solution)/shard_map/ppermute | solution.py:327
  8.2 4.3 %shard_map.65 = (bf16[2048,128]{1,0:T(8,128)(2,1)S(1)}, s32[8,128]{1,0:T(8,128)S(1)}, f32[2048,128]{1,0:T(8,128)S(1)}, f32[2048,256]{1,0:T(8,128)S(1)}, bf16[1024,4096]{1,0:T(8,128)(2,1)S(1)}) custom-call(s32[8]{0:T(128)} %order_hbm.1, s32[4]{0:T(128)} %docs_hbm.1, bf16[128,2048]{1,0:T(8,128)(2,1)} %q_hbm.1, bf16[2048,4096]{1,0:T(8,128)(2,1)} %w_hbm.3, ...), custom_call_target="tpu_custom_call" | custom-call | flops 4000000000 | tf_op jit(solution)/shard_map/pallas_call | solution.py:293
  12.5 5.6 %collective-permute-done.2.refs_2_ = bf16[256,256]{1,0:T(8,128)(2,1)S(1)} collective-permute-done((bf16[256,256]{1,0:T(8,128)(2,1)S(1)}, bf16[256,256]{1,0:T(8,128)(2,1)S(1)}, u32[]{:S(2)}, u32[]{:S(2)}) %collective-permute-start.2) | collective-permute-done | bytes 131104 | tf_op jit(solution)/shard_map/ppermute | solution.py:327
  18.0 0.5 %collective-permute-start.6 = (bf16[256,256]{1,0:T(8,128)(2,1)S(1)}, bf16[256,256]{1,0:T(8,128)(2,1)S(1)}, u32[]{:S(2)}, u32[]{:S(2)}) collective-permute-start(bf16[256,256]{1,0:T(8,128)(2,1)S(1)} %collective-permute-done.2.refs_2_), channel_id=1, source_target_pairs={{0,4},{4,0},{8,12},{12,8},{16,20},{20,16},{24,28},{28,24},{1,5},{5... | collective-permute-start | bytes 393224 | tf_op jit(solution)/shard_map/ppermute | solution.py:327
  18.6 0.0 collective-permute-start.5
  18.6 0.0 collective-permute-done.1.refs_1_
  18.6 1.5 %collective-permute-start.3 = (bf16[256,256]{1,0:T(8,128)(2,1)S(1)}, bf16[256,256]{1,0:T(8,128)(2,1)S(1)}, u32[]{:S(2)}, u32[]{:S(2)}) collective-permute-start(bf16[256,256]{1,0:T(8,128)(2,1)S(1)} %collective-permute-done.1.refs_1_), channel_id=1, source_target_pairs={{0,4},{4,0},{8,12},{12,8},{16,20},{20,16},{24,28},{28,24},{1,5},{5... | collective-permute-start | bytes 393224 | tf_op jit(solution)/shard_map/ppermute | solution.py:327
  20.1 0.0 collective-permute-done.refs_0_
  20.1 3.5 %shard_map.66 = (f32[2048,128]{1,0:T(8,128)S(1)}, f32[2048,256]{1,0:T(8,128)S(1)}, bf16[1024,4096]{1,0:T(8,128)(2,1)S(1)}) custom-call(s32[8,128]{1,0:T(8,128)S(1)} %get-tuple-element.20.seen_ref, bf16[2048,4096]{1,0:T(8,128)(2,1)} %w_hbm.3, bf16[2048,128]{1,0:T(8,128)(2,1)S(1)} %get-tuple-element.21.qr_ref, ...), custom_call_target="tpu_custom_call", output_to_operand_aliasing={{0}: (3, {}), {1}: (4, {})} | custom-call | flops 4000000000 | tf_op jit(solution)/shard_map/pallas_call | solution.py:293
  23.6 0.0 collective-permute-done.4.refs_1_
  23.6 0.0 collective-permute-done.5.refs_2_
  23.6 1.9 %collective-permute-done.3.refs_0_ = bf16[256,256]{1,0:T(8,128)(2,1)S(1)} collective-permute-done((bf16[256,256]{1,0:T(8,128)(2,1)S(1)}, bf16[256,256]{1,0:T(8,128)(2,1)S(1)}, u32[]{:S(2)}, u32[]{:S(2)}) %collective-permute-start.3) | collective-permute-done | bytes 131104 | tf_op jit(solution)/shard_map/ppermute | solution.py:327
  25.5 1.6 %shard_map.67 = (f32[2048,128]{1,0:T(8,128)S(1)}, f32[2048,256]{1,0:T(8,128)S(1)}) custom-call(s32[8,128]{1,0:T(8,128)S(1)} %get-tuple-element.20.seen_ref, bf16[2048,128]{1,0:T(8,128)(2,1)S(1)} %get-tuple-element.21.qr_ref, f32[2048,128]{1,0:T(8,128)S(1)} %get-tuple-element.24.top_in, ...), custom_call_target="tpu_custom_call", output_to_operand_aliasing={{0}: (2, {}), {1}: (3, {})} | custom-call | flops 1000000000 | tf_op jit(solution)/shard_map/pallas_call | solution.py:293
  27.1 0.0 collective-permute-done.6.refs_0_
  27.1 1.5 %shard_map.68 = (f32[2048,128]{1,0:T(8,128)S(1)}, f32[2048,256]{1,0:T(8,128)S(1)}, bf16[128,2048]{1,0:T(8,128)(2,1)S(1)}, bf16[64,2048]{1,0:T(8,128)(2,1)S(1)}, f32[64,2048]{1,0:T(8,128)S(1)}) custom-call(s32[8,128]{1,0:T(8,128)S(1)} %get-tuple-element.20.seen_ref, ...), custom_call_target="tpu_custom_call", output_to_operand_aliasing={{0}: (2, {}), {1}: (3, {})} | custom-call | flops 1073741824 | tf_op jit(solution)/shard_map/pallas_call | solution.py:293
  28.7 0.1 collective-permute-start.9
  28.8 1.3 %shard_map.69 = (bf16[64,2048]{1,0:T(8,128)(2,1)S(1)}, f32[64,2048]{1,0:T(8,128)S(1)}) custom-call(bf16[128,2048]{1,0:T(8,128)(2,1)S(1)} %get-tuple-element.30.att_ref, bf16[1024,4096]{1,0:T(8,128)(2,1)S(1)} %get-tuple-element.28.refs_1_.w0_ref, bf16[1024,4096]{1,0:T(8,128)(2,1)S(1)} %get-tuple-element.29.refs_2_.w1_ref), custom_call_target="tpu_custom_call" | custom-call | flops 1073741824 | tf_op jit(solution)/shard_map/pallas_call | solution.py:293
  30.1 0.6 %collective-permute-start.7 = (bf16[64,2048]{1,0:T(8,128)(2,1)S(1)}, bf16[64,2048]{1,0:T(8,128)(2,1)S(1)}, u32[]{:S(2)}, u32[]{:S(2)}) collective-permute-start(bf16[64,2048]{1,0:T(8,128)(2,1)S(1)} %get-tuple-element.32), channel_id=1, source_target_pairs={{0,1},{1,0},{2,3},{3,2},{4,5},{5,4},{6,7},{7,6},{8,9},{9,8},{10,11... | collective-permute-start | bytes 786440 | tf_op jit(solution)/shard_map/ppermute | solution.py:372
  30.6 0.0 collective-permute-done.9.other_ref
  30.7 1.6 %collective-permute-start.10 = (bf16[32,2048]{1,0:T(8,128)(2,1)S(1)}, bf16[32,2048]{1,0:T(8,128)(2,1)S(1)}, u32[]{:S(2)}, u32[]{:S(2)}) collective-permute-start(bf16[32,2048]{1,0:T(8,128)(2,1)S(1)} %add_convert_fusion), channel_id=1, source_target_pairs={{0,2},{1,3},{2,0},{3,1},{4,6},{5,7},{6,4},{7,5},{8,10},{9,11},{10,... | collective-permute-start | bytes 393224 | tf_op jit(solution)/shard_map/ppermute | solution.py:372
  32.3 0.0 collective-permute-done.7.other_ref
  32.3 1.1 %collective-permute-start.8 = (bf16[32,2048]{1,0:T(8,128)(2,1)S(1)}, bf16[32,2048]{1,0:T(8,128)(2,1)S(1)}, u32[]{:S(2)}, u32[]{:S(2)}) collective-permute-start(bf16[32,2048]{1,0:T(8,128)(2,1)S(1)} %add_convert_fusion.1), channel_id=1, source_target_pairs={{0,2},{1,3},{2,0},{3,1},{4,6},{5,7},{6,4},{7,5},{8,10},{9,11},{10,... | collective-permute-start | bytes 393224 | tf_op jit(solution)/shard_map/ppermute | solution.py:372
  33.4 3.7 %collective-permute-done.10.crossed_ref = bf16[32,2048]{1,0:T(8,128)(2,1)S(1)} collective-permute-done((bf16[32,2048]{1,0:T(8,128)(2,1)S(1)}, bf16[32,2048]{1,0:T(8,128)(2,1)S(1)}, u32[]{:S(2)}, u32[]{:S(2)}) %collective-permute-start.10) | collective-permute-done | bytes 131104 | tf_op jit(solution)/shard_map/ppermute | solution.py:372
  37.1 0.7 %shard_map.70.refs_0_ = bf16[32,4096]{1,0:T(8,128)(2,1)} custom-call(f32[64,2048]{1,0:T(8,128)S(1)} %get-tuple-element.33.keep_ref, bf16[64,2048]{1,0:T(8,128)(2,1)S(1)} %collective-permute-done.9.other_ref, bf16[32,2048]{1,0:T(8,128)(2,1)S(1)} %collective-permute-done.10.crossed_ref), custom_call_target="tpu_custom_call" | custom-call | tf_op jit(solution)/shard_map/pallas_call | solution.py:386
  37.8 1.1 %collective-permute-done.8.crossed_ref = bf16[32,2048]{1,0:T(8,128)(2,1)S(1)} collective-permute-done((bf16[32,2048]{1,0:T(8,128)(2,1)S(1)}, bf16[32,2048]{1,0:T(8,128)(2,1)S(1)}, u32[]{:S(2)}, u32[]{:S(2)}) %collective-permute-start.8) | collective-permute-done | bytes 131104 | tf_op jit(solution)/shard_map/ppermute | solution.py:372
  39.0 0.7 %shard_map.71 = bf16[32,4096]{1,0:T(8,128)(2,1)} custom-call(f32[64,2048]{1,0:T(8,128)S(1)} %get-tuple-element.31.keep_ref, bf16[64,2048]{1,0:T(8,128)(2,1)S(1)} %collective-permute-done.7.other_ref, bf16[32,2048]{1,0:T(8,128)(2,1)S(1)} %collective-permute-done.8.crossed_ref, bf16[32,4096]{1,0:T(8,128)(2,1)} %shard_map.70.refs_0_), custom_call_target="tpu_custom_call", output_to_operand_aliasing={{}: (3, {})} | custom-call | tf_op jit(solution)/shard_map/pallas_call | solution.py:386
  (2 shorter events, 0.1 us)
Async XLA Ops:
  0.9 22.7 %collective-permute-start.4 = (bf16[256,256]{1,0:T(8,128)(2,1)S(1)}, bf16[256,256]{1,0:T(8,128)(2,1)S(1)}, u32[]{:S(2)}, u32[]{:S(2)}) collective-permute-start(bf16[256,256]{1,0:T(8,128)(2,1)S(1)} %shard_map.64.kv_ref), channel_id=1, source_target_pairs={{0,28},{4,24},{8,20},{12,16},{16,12},{20,8},{24,4},{28,0},{1,29},{... | collective-permute-start | bytes 393224 | tf_op jit(solution)/shard_map/ppermute | solution.py:327
  7.0 11.1 %collective-permute-start.2 = (bf16[256,256]{1,0:T(8,128)(2,1)S(1)}, bf16[256,256]{1,0:T(8,128)(2,1)S(1)}, u32[]{:S(2)}, u32[]{:S(2)}) collective-permute-start(bf16[256,256]{1,0:T(8,128)(2,1)S(1)} %shard_map.64.kv_ref), channel_id=1, source_target_pairs={{0,16},{4,20},{8,24},{12,28},{16,0},{20,4},{24,8},{28,12},{1,17},{... | collective-permute-start | bytes 393224 | tf_op jit(solution)/shard_map/ppermute | solution.py:327
  7.0 11.6 %collective-permute-start.1 = (bf16[256,256]{1,0:T(8,128)(2,1)S(1)}, bf16[256,256]{1,0:T(8,128)(2,1)S(1)}, u32[]{:S(2)}, u32[]{:S(2)}) collective-permute-start(bf16[256,256]{1,0:T(8,128)(2,1)S(1)} %shard_map.64.kv_ref), channel_id=1, source_target_pairs={{0,8},{4,12},{8,0},{12,4},{16,24},{20,28},{24,16},{28,20},{1,9},{5... | collective-permute-start | bytes 393224 | tf_op jit(solution)/shard_map/ppermute | solution.py:327
  7.8 12.3 %collective-permute-start = (bf16[256,256]{1,0:T(8,128)(2,1)S(1)}, bf16[256,256]{1,0:T(8,128)(2,1)S(1)}, u32[]{:S(2)}, u32[]{:S(2)}) collective-permute-start(bf16[256,256]{1,0:T(8,128)(2,1)S(1)} %shard_map.64.kv_ref), channel_id=1, source_target_pairs={{0,4},{4,0},{8,12},{12,8},{16,20},{20,16},{24,28},{28,24},{1,5},{5... | collective-permute-start | bytes 393224 | tf_op jit(solution)/shard_map/ppermute | solution.py:327
  18.0 9.1 %collective-permute-start.6 = (bf16[256,256]{1,0:T(8,128)(2,1)S(1)}, bf16[256,256]{1,0:T(8,128)(2,1)S(1)}, u32[]{:S(2)}, u32[]{:S(2)}) collective-permute-start(bf16[256,256]{1,0:T(8,128)(2,1)S(1)} %collective-permute-done.2.refs_2_), channel_id=1, source_target_pairs={{0,4},{4,0},{8,12},{12,8},{16,20},{20,16},{24,28},{28,24},{1,5},{5... | collective-permute-start | bytes 393224 | tf_op jit(solution)/shard_map/ppermute | solution.py:327
  18.6 5.0 %collective-permute-start.5 = (bf16[256,256]{1,0:T(8,128)(2,1)S(1)}, bf16[256,256]{1,0:T(8,128)(2,1)S(1)}, u32[]{:S(2)}, u32[]{:S(2)}) collective-permute-start(bf16[256,256]{1,0:T(8,128)(2,1)S(1)} %collective-permute-done.2.refs_2_), channel_id=1, source_target_pairs={{0,8},{4,12},{8,0},{12,4},{16,24},{20,28},{24,16},{28,20},{1,9},{5... | collective-permute-start | bytes 393224 | tf_op jit(solution)/shard_map/ppermute | solution.py:327
  18.6 6.9 %collective-permute-start.3 = (bf16[256,256]{1,0:T(8,128)(2,1)S(1)}, bf16[256,256]{1,0:T(8,128)(2,1)S(1)}, u32[]{:S(2)}, u32[]{:S(2)}) collective-permute-start(bf16[256,256]{1,0:T(8,128)(2,1)S(1)} %collective-permute-done.1.refs_1_), channel_id=1, source_target_pairs={{0,4},{4,0},{8,12},{12,8},{16,20},{20,16},{24,28},{28,24},{1,5},{5... | collective-permute-start | bytes 393224 | tf_op jit(solution)/shard_map/ppermute | solution.py:327
  28.7 2.0 %collective-permute-start.9 = (bf16[64,2048]{1,0:T(8,128)(2,1)S(1)}, bf16[64,2048]{1,0:T(8,128)(2,1)S(1)}, u32[]{:S(2)}, u32[]{:S(2)}) collective-permute-start(bf16[64,2048]{1,0:T(8,128)(2,1)S(1)} %get-tuple-element.34), channel_id=1, source_target_pairs={{0,1},{1,0},{2,3},{3,2},{4,5},{5,4},{6,7},{7,6},{8,9},{9,8},{10,11... | collective-permute-start | bytes 786440 | tf_op jit(solution)/shard_map/ppermute | solution.py:372
  30.1 2.2 %collective-permute-start.7 = (bf16[64,2048]{1,0:T(8,128)(2,1)S(1)}, bf16[64,2048]{1,0:T(8,128)(2,1)S(1)}, u32[]{:S(2)}, u32[]{:S(2)}) collective-permute-start(bf16[64,2048]{1,0:T(8,128)(2,1)S(1)} %get-tuple-element.32), channel_id=1, source_target_pairs={{0,1},{1,0},{2,3},{3,2},{4,5},{5,4},{6,7},{7,6},{8,9},{9,8},{10,11... | collective-permute-start | bytes 786440 | tf_op jit(solution)/shard_map/ppermute | solution.py:372
  30.7 6.4 %collective-permute-start.10 = (bf16[32,2048]{1,0:T(8,128)(2,1)S(1)}, bf16[32,2048]{1,0:T(8,128)(2,1)S(1)}, u32[]{:S(2)}, u32[]{:S(2)}) collective-permute-start(bf16[32,2048]{1,0:T(8,128)(2,1)S(1)} %add_convert_fusion), channel_id=1, source_target_pairs={{0,2},{1,3},{2,0},{3,1},{4,6},{5,7},{6,4},{7,5},{8,10},{9,11},{10,... | collective-permute-start | bytes 393224 | tf_op jit(solution)/shard_map/ppermute | solution.py:372
  32.3 6.7 %collective-permute-start.8 = (bf16[32,2048]{1,0:T(8,128)(2,1)S(1)}, bf16[32,2048]{1,0:T(8,128)(2,1)S(1)}, u32[]{:S(2)}, u32[]{:S(2)}) collective-permute-start(bf16[32,2048]{1,0:T(8,128)(2,1)S(1)} %add_convert_fusion.1), channel_id=1, source_target_pairs={{0,2},{1,3},{2,0},{3,1},{4,6},{5,7},{6,4},{7,5},{8,10},{9,11},{10,... | collective-permute-start | bytes 393224 | tf_op jit(solution)/shard_map/ppermute | solution.py:372

commit v5 on v4

--- a/solution.py
+++ b/solution.py
@@ -223,17 +223,12 @@
                 sweep(qr_ref, top_ref, sum_ref, [kv_ref.at[first + i] for i in range(count)], None)
 
 
-def more(slots, seen_ref, w_hbm, qr_ref, top_in, sum_in, *refs):
+def more(slots, first, seen_ref, w_hbm, qr_ref, top_in, sum_in, *refs):
     kv_refs, (top_ref, sum_ref, w_ref, kv_ref, w_sems) = (
         refs[: len(slots)], refs[len(slots) :])
-    loads = load_rows(w_hbm, w_ref.shape[0], w_ref, w_sems)
+    loads = load_rows(w_hbm, first, w_ref, w_sems)
     seen_blocks(slots, seen_ref, qr_ref, top_ref, sum_ref, kv_refs, kv_ref)
     wait_all(loads)
-
-
-def again(slots, seen_ref, qr_ref, top_in, sum_in, *refs):
-    kv_refs, (top_ref, sum_ref, kv_ref) = refs[: len(slots)], refs[len(slots) :]
-    seen_blocks(slots, seen_ref, qr_ref, top_ref, sum_ref, kv_refs, kv_ref)
 
 
 def project(att_ref, w_refs, first, chunk, give_ref, keep_ref):
@@ -252,8 +247,8 @@
 
 
 def finish(slots, chunk, seen_ref, qr_ref, top_in, sum_in, *refs):
-    kv_refs, (w0_ref, w1_ref, top_ref, sum_ref, att_ref, give_ref, keep_ref, kv_ref) = (
-        refs[: len(slots)], refs[len(slots) :])
+    kv_refs, w_refs, (top_ref, sum_ref, att_ref, give_ref, keep_ref, kv_ref) = (
+        refs[: len(slots)], refs[len(slots) : -6], refs[-6:])
     seen_blocks(slots, seen_ref, qr_ref, top_ref, sum_ref, kv_refs, kv_ref)
     rows, width = att_ref.shape
     for h in range(width // HEAD_SIZE):
@@ -261,11 +256,12 @@
         att_ref[:, h * HEAD_SIZE : (h + 1) * HEAD_SIZE] = (
             sum_ref[at, :HEAD_SIZE] * pl.reciprocal(sum_ref[at, HEAD_SIZE:])
         ).astype(jnp.bfloat16)
-    project(att_ref, (w0_ref, w1_ref), 0, chunk, give_ref, keep_ref)
-
-
-def rest(chunk, att_ref, w0_ref, w1_ref, give_ref, keep_ref):
-    project(att_ref, (w0_ref, w1_ref), w0_ref.shape[1] - give_ref.shape[1], chunk, give_ref, keep_ref)
+    project(att_ref, w_refs, 0, chunk, give_ref, keep_ref)
+
+
+def rest(chunk, att_ref, *refs):
+    w_refs, (give_ref, keep_ref) = refs[:-2], refs[-2:]
+    project(att_ref, w_refs, w_refs[0].shape[1] - give_ref.shape[1], chunk, give_ref, keep_ref)
 
 
 def last(at, keep_ref, other_ref, crossed_ref, *refs):
@@ -314,6 +310,7 @@
         copy.wait()
 
 
+SHARES = (3, 4, 1)
 PLAN = ((4, 0, 4), (2, 0, 2), (1, 0, 1), (7, 0, 7), (3, 2, 1), (6, 4, 2), (5, 4, 1))
 
 
@@ -334,37 +331,35 @@
         got[s] = swap(got[via], hop)
 
     states = [((heads * rows, HEAD_SIZE), f32), ((heads * rows, 2 * HEAD_SIZE), f32)]
-    half_weight = ((width // 2, out_width), bf16)
+    split = [width * share // 8 for share in SHARES]
     dma = pltpu.SemaphoreType.DMA
-    qr, seen, top, sums, weight0 = kernel(
+    qr, seen, top, sums, weight = kernel(
         functools.partial(begin, n_tp),
         [("hbm", block_order), ("hbm", doc_blocks), ("hbm", queries), ("hbm", out_weight), ("vmem", kv)],
-        [((heads * rows, HEAD_SIZE), bf16), ((n, HEAD_SIZE), jnp.int32)] + states + [half_weight],
+        [((heads * rows, HEAD_SIZE), bf16), ((n, HEAD_SIZE), jnp.int32)] + states + [((split[0], out_width), bf16)],
         [pltpu.VMEM((rows, width), bf16), pltpu.SMEM(block_order.shape, jnp.int32),
-         pltpu.SMEM(doc_blocks.shape, jnp.int32), dma((3,)), dma((8,))],
+         pltpu.SMEM(doc_blocks.shape, jnp.int32), dma((3,)), dma((split[0] // 128,))],
         flops=4 * 10**9, limit=8)
 
     def held(slots):
         return pltpu.VMEM((min(len(slots), n // 2 - 1),) + kv.shape, bf16)
 
-    slots = (1, 2, 4)
-    top, sums, weight1 = kernel(
-        functools.partial(more, slots),
-        [("vmem", seen), ("hbm", out_weight)]
-        + [("vmem", x) for x in (qr, top, sums, *(got[s] for s in slots))],
-        states + [half_weight], [held(slots), dma((8,))],
-        flops=4 * 10**9, aliases={3: 0, 4: 1}, limit=8)
-    slots = (3, 7, 6)
-    top, sums = kernel(
-        functools.partial(again, slots),
-        [("vmem", x) for x in (seen, qr, top, sums, *(got[s] for s in slots))],
-        states, [held(slots)], flops=10**9, aliases={2: 0, 3: 1}, limit=8)
+    weights = [weight]
+    for slots, depth in zip(((1, 2, 4), (3, 7, 6)), split[1:]):
+        first = sum(w.shape[0] for w in weights)
+        top, sums, weight = kernel(
+            functools.partial(more, slots, first),
+            [("vmem", seen), ("hbm", out_weight)]
+            + [("vmem", x) for x in (qr, top, sums, *(got[s] for s in slots))],
+            states + [((depth, out_width), bf16)], [held(slots), dma((depth // 128,))],
+            flops=4 * 10**9, aliases={3: 0, 4: 1}, limit=8)
+        weights.append(weight)
     slots = (5,)
     part, chunk, half = rows // n_tp, 512, out_width // 2
     shares = [((rows // 2, half), bf16), ((rows // 2, half), f32)]
     _, _, att, give0, keep0 = kernel(
         functools.partial(finish, slots, chunk),
-        [("vmem", x) for x in (seen, qr, top, sums, *(got[s] for s in slots), weight0, weight1)],
+        [("vmem", x) for x in (seen, qr, top, sums, *(got[s] for s in slots), *weights)],
         states + [((rows, width), bf16)] + shares, [held(slots)],
         flops=rows * width * out_width, aliases={2: 0, 3: 1}, limit=8)
 
@@ -373,7 +368,7 @@
 
     got0 = across(give0, 1)
     give1, keep1 = kernel(
-        functools.partial(rest, chunk), [("vmem", x) for x in (att, weight0, weight1)],
+        functools.partial(rest, chunk), [("vmem", x) for x in (att, *weights)],
         shares, flops=rows * width * out_width, limit=8)
     got1 = across(give1, 1)
     crossed = []

time: 39.8 us -> 39.8 us (level)
  Pallas kernels: 14.6 us -> 13.9 us
  waiting for transfers between devices: 12.3 us -> 12.9 us
    pallas_call x6, Pallas kernels: 13.1 us -> 12.5 us  [kernel(): pl.pallas_call(body, out_shape=tuple((pltpu.VMEM(shape, dtype) for shape,...]
    ppermute x7, waiting for transfers between devices: 7.47 us -> 8.09 us  [swap(): return lax.ppermute(block, 'cp', [(i, i ^ s) for i in range(n)])]
  transfers between devices with their start and end apart: 11 -> 11, of which waited for: 4 -> 4; matrix products, arithmetic and copies ran while one was open for 0% -> 0% of each run, Pallas kernels for 29% -> 27%
where the time goes in v5:
time: 39.8 us; the launch traced here: 39.6 us
  Pallas kernels  13.9 us (35%)
  waiting for transfers between devices  12.9 us (32%)
  starting transfers between devices  12.7 us (32%)
    pallas_call x6, Pallas kernels, kernel(): pl.pallas_call(body, out_shape=tuple((pltpu.VMEM(shape, dtype) for shape,...  12.5 us
    ppermute x7, starting transfers between devices, swap(): return lax.ppermute(block, 'cp', [(i, i ^ s) for i in range(n)])  9.31 us
    ppermute x7, waiting for transfers between devices, swap(): return lax.ppermute(block, 'cp', [(i, i ^ s) for i in range(n)])  8.09 us
    ppermute x4, waiting for transfers between devices, across(): return lax.ppermute(x, 'tp', [(i, i ^ hop) for i in range(n_tp)])  4.85 us
    ppermute x4, starting transfers between devices, across(): return lax.ppermute(x, 'tp', [(i, i ^ hop) for i in range(n_tp)])  3.35 us
    pallas_call x2, Pallas kernels, blockwise(): pl.pallas_call(functools.partial(last, i * half), out_shape=(pltpu.HBM((p...  1.41 us
  transfers between devices with their start and end apart: 11, of which 4 were waited for; matrix products, arithmetic and copies ran while one was open for 0% of the time, Pallas kernels for 27%

profile of v5, /device:TPU:0, one launch (start us, length us, event | category | flops | bytes accessed | tf_op | source)
XLA Modules:
  0.0 39.6 jit_solution(8694407488829969470)
XLA Ops:
  0.0 0.9 %shard_map.64.kv_ref = bf16[256,256]{1,0:T(8,128)(2,1)S(1)} custom-call(bf16[128,256]{1,0:T(8,128)(2,1)} %k_hbm.1, bf16[128,256]{1,0:T(8,128)(2,1)} %v_hbm.1), custom_call_target="tpu_custom_call" | custom-call | tf_op jit(solution)/shard_map/pallas_call | solution.py:289
  0.9 6.1 %collective-permute-start.4 = (bf16[256,256]{1,0:T(8,128)(2,1)S(1)}, bf16[256,256]{1,0:T(8,128)(2,1)S(1)}, u32[]{:S(2)}, u32[]{:S(2)}) collective-permute-start(bf16[256,256]{1,0:T(8,128)(2,1)S(1)} %shard_map.64.kv_ref), channel_id=1, source_target_pairs={{0,28},{4,24},{8,20},{12,16},{16,12},{20,8},{24,4},{28,0},{1,29},{... | collective-permute-start | bytes 393224 | tf_op jit(solution)/shard_map/ppermute | solution.py:324
  7.0 0.0 collective-permute-start.2
  7.0 0.8 %collective-permute-start.1 = (bf16[256,256]{1,0:T(8,128)(2,1)S(1)}, bf16[256,256]{1,0:T(8,128)(2,1)S(1)}, u32[]{:S(2)}, u32[]{:S(2)}) collective-permute-start(bf16[256,256]{1,0:T(8,128)(2,1)S(1)} %shard_map.64.kv_ref), channel_id=1, source_target_pairs={{0,8},{4,12},{8,0},{12,4},{16,24},{20,28},{24,16},{28,20},{1,9},{5... | collective-permute-start | bytes 393224 | tf_op jit(solution)/shard_map/ppermute | solution.py:324
  7.8 0.4 %collective-permute-start = (bf16[256,256]{1,0:T(8,128)(2,1)S(1)}, bf16[256,256]{1,0:T(8,128)(2,1)S(1)}, u32[]{:S(2)}, u32[]{:S(2)}) collective-permute-start(bf16[256,256]{1,0:T(8,128)(2,1)S(1)} %shard_map.64.kv_ref), channel_id=1, source_target_pairs={{0,4},{4,0},{8,12},{12,8},{16,20},{20,16},{24,28},{28,24},{1,5},{5... | collective-permute-start | bytes 393224 | tf_op jit(solution)/shard_map/ppermute | solution.py:324
  8.2 3.7 %shard_map.65 = (bf16[2048,128]{1,0:T(8,128)(2,1)S(1)}, s32[8,128]{1,0:T(8,128)S(1)}, f32[2048,128]{1,0:T(8,128)S(1)}, f32[2048,256]{1,0:T(8,128)S(1)}, bf16[768,4096]{1,0:T(8,128)(2,1)S(1)}) custom-call(s32[8]{0:T(128)} %order_hbm.1, s32[4]{0:T(128)} %docs_hbm.1, bf16[128,2048]{1,0:T(8,128)(2,1)} %q_hbm.1, bf16[2048,4096]{1,0:T(8,128)(2,1)} %w_hbm.5, ...), custom_call_target="tpu_custom_call" | custom-call | flops 4000000000 | tf_op jit(solution)/shard_map/pallas_call | solution.py:289
  11.9 6.2 %collective-permute-done.2.refs_2_ = bf16[256,256]{1,0:T(8,128)(2,1)S(1)} collective-permute-done((bf16[256,256]{1,0:T(8,128)(2,1)S(1)}, bf16[256,256]{1,0:T(8,128)(2,1)S(1)}, u32[]{:S(2)}, u32[]{:S(2)}) %collective-permute-start.2) | collective-permute-done | bytes 131104 | tf_op jit(solution)/shard_map/ppermute | solution.py:324
  18.0 0.5 %collective-permute-start.6 = (bf16[256,256]{1,0:T(8,128)(2,1)S(1)}, bf16[256,256]{1,0:T(8,128)(2,1)S(1)}, u32[]{:S(2)}, u32[]{:S(2)}) collective-permute-start(bf16[256,256]{1,0:T(8,128)(2,1)S(1)} %collective-permute-done.2.refs_2_), channel_id=1, source_target_pairs={{0,4},{4,0},{8,12},{12,8},{16,20},{20,16},{24,28},{28,24},{1,5},{5... | collective-permute-start | bytes 393224 | tf_op jit(solution)/shard_map/ppermute | solution.py:324
  18.6 0.0 collective-permute-start.5
  18.6 0.0 collective-permute-done.1.refs_1_
  18.6 1.5 %collective-permute-start.3 = (bf16[256,256]{1,0:T(8,128)(2,1)S(1)}, bf16[256,256]{1,0:T(8,128)(2,1)S(1)}, u32[]{:S(2)}, u32[]{:S(2)}) collective-permute-start(bf16[256,256]{1,0:T(8,128)(2,1)S(1)} %collective-permute-done.1.refs_1_), channel_id=1, source_target_pairs={{0,4},{4,0},{8,12},{12,8},{16,20},{20,16},{24,28},{28,24},{1,5},{5... | collective-permute-start | bytes 393224 | tf_op jit(solution)/shard_map/ppermute | solution.py:324
  20.1 0.0 collective-permute-done.refs_0_
  20.1 3.5 %shard_map.66 = (f32[2048,128]{1,0:T(8,128)S(1)}, f32[2048,256]{1,0:T(8,128)S(1)}, bf16[1024,4096]{1,0:T(8,128)(2,1)S(1)}) custom-call(s32[8,128]{1,0:T(8,128)S(1)} %get-tuple-element.21.seen_ref, bf16[2048,4096]{1,0:T(8,128)(2,1)} %w_hbm.5, bf16[2048,128]{1,0:T(8,128)(2,1)S(1)} %get-tuple-element.22.qr_ref, ...), custom_call_target="tpu_custom_call", output_to_operand_aliasing={{0}: (3, {}), {1}: (4, {})} | custom-call | flops 4000000000 | tf_op jit(solution)/shard_map/pallas_call | solution.py:289
  23.6 0.0 collective-permute-done.4.refs_1_
  23.6 0.0 collective-permute-done.5.refs_2_
  23.6 1.9 %collective-permute-done.3.refs_0_ = bf16[256,256]{1,0:T(8,128)(2,1)S(1)} collective-permute-done((bf16[256,256]{1,0:T(8,128)(2,1)S(1)}, bf16[256,256]{1,0:T(8,128)(2,1)S(1)}, u32[]{:S(2)}, u32[]{:S(2)}) %collective-permute-start.3) | collective-permute-done | bytes 131104 | tf_op jit(solution)/shard_map/ppermute | solution.py:324
  25.5 1.6 %shard_map.67 = (f32[2048,128]{1,0:T(8,128)S(1)}, f32[2048,256]{1,0:T(8,128)S(1)}, bf16[256,4096]{1,0:T(8,128)(2,1)S(1)}) custom-call(s32[8,128]{1,0:T(8,128)S(1)} %get-tuple-element.21.seen_ref, bf16[2048,4096]{1,0:T(8,128)(2,1)} %w_hbm.5, bf16[2048,128]{1,0:T(8,128)(2,1)S(1)} %get-tuple-element.22.qr_ref, ...), custom_call_target="tpu_custom_call", output_to_operand_aliasing={{0}: (3, {}), {1}: (4, {})} | custom-call | flops 4000000000 | tf_op jit(solution)/shard_map/pallas_call | solution.py:289
  27.1 0.0 collective-permute-done.6.refs_0_
  27.1 1.5 %shard_map.68 = (f32[2048,128]{1,0:T(8,128)S(1)}, f32[2048,256]{1,0:T(8,128)S(1)}, bf16[128,2048]{1,0:T(8,128)(2,1)S(1)}, bf16[64,2048]{1,0:T(8,128)(2,1)S(1)}, f32[64,2048]{1,0:T(8,128)S(1)}) custom-call(s32[8,128]{1,0:T(8,128)S(1)} %get-tuple-element.21.seen_ref, ...), custom_call_target="tpu_custom_call", output_to_operand_aliasing={{0}: (2, {}), {1}: (3, {})} | custom-call | flops 1073741824 | tf_op jit(solution)/shard_map/pallas_call | solution.py:289
  28.6 0.1 collective-permute-start.9
  28.7 1.3 %shard_map.69 = (bf16[64,2048]{1,0:T(8,128)(2,1)S(1)}, f32[64,2048]{1,0:T(8,128)S(1)}) custom-call(bf16[128,2048]{1,0:T(8,128)(2,1)S(1)} %get-tuple-element.32.att_ref, bf16[768,4096]{1,0:T(8,128)(2,1)S(1)} %get-tuple-element.29.refs_1_.refs_0_, bf16[1024,4096]{1,0:T(8,128)(2,1)S(1)} %get-tuple-element.30.refs_2_.refs_1_, ...), custom_call_target="tpu_custom_call" | custom-call | flops 1073741824 | tf_op jit(solution)/shard_map/pallas_call | solution.py:289
  30.0 0.6 %collective-permute-start.7 = (bf16[64,2048]{1,0:T(8,128)(2,1)S(1)}, bf16[64,2048]{1,0:T(8,128)(2,1)S(1)}, u32[]{:S(2)}, u32[]{:S(2)}) collective-permute-start(bf16[64,2048]{1,0:T(8,128)(2,1)S(1)} %get-tuple-element.34), channel_id=1, source_target_pairs={{0,1},{1,0},{2,3},{3,2},{4,5},{5,4},{6,7},{7,6},{8,9},{9,8},{10,11... | collective-permute-start | bytes 786440 | tf_op jit(solution)/shard_map/ppermute | solution.py:367
  30.6 0.0 collective-permute-done.9.other_ref
  30.6 1.6 %collective-permute-start.10 = (bf16[32,2048]{1,0:T(8,128)(2,1)S(1)}, bf16[32,2048]{1,0:T(8,128)(2,1)S(1)}, u32[]{:S(2)}, u32[]{:S(2)}) collective-permute-start(bf16[32,2048]{1,0:T(8,128)(2,1)S(1)} %add_convert_fusion), channel_id=1, source_target_pairs={{0,2},{1,3},{2,0},{3,1},{4,6},{5,7},{6,4},{7,5},{8,10},{9,11},{10,... | collective-permute-start | bytes 393224 | tf_op jit(solution)/shard_map/ppermute | solution.py:367
  32.2 0.0 collective-permute-done.7.other_ref
  32.2 1.1 %collective-permute-start.8 = (bf16[32,2048]{1,0:T(8,128)(2,1)S(1)}, bf16[32,2048]{1,0:T(8,128)(2,1)S(1)}, u32[]{:S(2)}, u32[]{:S(2)}) collective-permute-start(bf16[32,2048]{1,0:T(8,128)(2,1)S(1)} %add_convert_fusion.1), channel_id=1, source_target_pairs={{0,2},{1,3},{2,0},{3,1},{4,6},{5,7},{6,4},{7,5},{8,10},{9,11},{10,... | collective-permute-start | bytes 393224 | tf_op jit(solution)/shard_map/ppermute | solution.py:367
  33.4 3.7 %collective-permute-done.10.crossed_ref = bf16[32,2048]{1,0:T(8,128)(2,1)S(1)} collective-permute-done((bf16[32,2048]{1,0:T(8,128)(2,1)S(1)}, bf16[32,2048]{1,0:T(8,128)(2,1)S(1)}, u32[]{:S(2)}, u32[]{:S(2)}) %collective-permute-start.10) | collective-permute-done | bytes 131104 | tf_op jit(solution)/shard_map/ppermute | solution.py:367
  37.0 0.7 %shard_map.70.refs_0_ = bf16[32,4096]{1,0:T(8,128)(2,1)} custom-call(f32[64,2048]{1,0:T(8,128)S(1)} %get-tuple-element.35.keep_ref, bf16[64,2048]{1,0:T(8,128)(2,1)S(1)} %collective-permute-done.9.other_ref, bf16[32,2048]{1,0:T(8,128)(2,1)S(1)} %collective-permute-done.10.crossed_ref), custom_call_target="tpu_custom_call" | custom-call | tf_op jit(solution)/shard_map/pallas_call | solution.py:381
  37.8 1.2 %collective-permute-done.8.crossed_ref = bf16[32,2048]{1,0:T(8,128)(2,1)S(1)} collective-permute-done((bf16[32,2048]{1,0:T(8,128)(2,1)S(1)}, bf16[32,2048]{1,0:T(8,128)(2,1)S(1)}, u32[]{:S(2)}, u32[]{:S(2)}) %collective-permute-start.8) | collective-permute-done | bytes 131104 | tf_op jit(solution)/shard_map/ppermute | solution.py:367
  38.9 0.7 %shard_map.71 = bf16[32,4096]{1,0:T(8,128)(2,1)} custom-call(f32[64,2048]{1,0:T(8,128)S(1)} %get-tuple-element.33.keep_ref, bf16[64,2048]{1,0:T(8,128)(2,1)S(1)} %collective-permute-done.7.other_ref, bf16[32,2048]{1,0:T(8,128)(2,1)S(1)} %collective-permute-done.8.crossed_ref, bf16[32,4096]{1,0:T(8,128)(2,1)} %shard_map.70.refs_0_), custom_call_target="tpu_custom_call", output_to_operand_aliasing={{}: (3, {})} | custom-call | tf_op jit(solution)/shard_map/pallas_call | solution.py:381
  (2 shorter events, 0.1 us)
Async XLA Ops:
  0.9 22.7 %collective-permute-start.4 = (bf16[256,256]{1,0:T(8,128)(2,1)S(1)}, bf16[256,256]{1,0:T(8,128)(2,1)S(1)}, u32[]{:S(2)}, u32[]{:S(2)}) collective-permute-start(bf16[256,256]{1,0:T(8,128)(2,1)S(1)} %shard_map.64.kv_ref), channel_id=1, source_target_pairs={{0,28},{4,24},{8,20},{12,16},{16,12},{20,8},{24,4},{28,0},{1,29},{... | collective-permute-start | bytes 393224 | tf_op jit(solution)/shard_map/ppermute | solution.py:324
  7.0 11.1 %collective-permute-start.2 = (bf16[256,256]{1,0:T(8,128)(2,1)S(1)}, bf16[256,256]{1,0:T(8,128)(2,1)S(1)}, u32[]{:S(2)}, u32[]{:S(2)}) collective-permute-start(bf16[256,256]{1,0:T(8,128)(2,1)S(1)} %shard_map.64.kv_ref), channel_id=1, source_target_pairs={{0,16},{4,20},{8,24},{12,28},{16,0},{20,4},{24,8},{28,12},{1,17},{... | collective-permute-start | bytes 393224 | tf_op jit(solution)/shard_map/ppermute | solution.py:324
  7.0 11.6 %collective-permute-start.1 = (bf16[256,256]{1,0:T(8,128)(2,1)S(1)}, bf16[256,256]{1,0:T(8,128)(2,1)S(1)}, u32[]{:S(2)}, u32[]{:S(2)}) collective-permute-start(bf16[256,256]{1,0:T(8,128)(2,1)S(1)} %shard_map.64.kv_ref), channel_id=1, source_target_pairs={{0,8},{4,12},{8,0},{12,4},{16,24},{20,28},{24,16},{28,20},{1,9},{5... | collective-permute-start | bytes 393224 | tf_op jit(solution)/shard_map/ppermute | solution.py:324
  7.8 12.3 %collective-permute-start = (bf16[256,256]{1,0:T(8,128)(2,1)S(1)}, bf16[256,256]{1,0:T(8,128)(2,1)S(1)}, u32[]{:S(2)}, u32[]{:S(2)}) collective-permute-start(bf16[256,256]{1,0:T(8,128)(2,1)S(1)} %shard_map.64.kv_ref), channel_id=1, source_target_pairs={{0,4},{4,0},{8,12},{12,8},{16,20},{20,16},{24,28},{28,24},{1,5},{5... | collective-permute-start | bytes 393224 | tf_op jit(solution)/shard_map/ppermute | solution.py:324
  18.0 9.1 %collective-permute-start.6 = (bf16[256,256]{1,0:T(8,128)(2,1)S(1)}, bf16[256,256]{1,0:T(8,128)(2,1)S(1)}, u32[]{:S(2)}, u32[]{:S(2)}) collective-permute-start(bf16[256,256]{1,0:T(8,128)(2,1)S(1)} %collective-permute-done.2.refs_2_), channel_id=1, source_target_pairs={{0,4},{4,0},{8,12},{12,8},{16,20},{20,16},{24,28},{28,24},{1,5},{5... | collective-permute-start | bytes 393224 | tf_op jit(solution)/shard_map/ppermute | solution.py:324
  18.6 5.0 %collective-permute-start.5 = (bf16[256,256]{1,0:T(8,128)(2,1)S(1)}, bf16[256,256]{1,0:T(8,128)(2,1)S(1)}, u32[]{:S(2)}, u32[]{:S(2)}) collective-permute-start(bf16[256,256]{1,0:T(8,128)(2,1)S(1)} %collective-permute-done.2.refs_2_), channel_id=1, source_target_pairs={{0,8},{4,12},{8,0},{12,4},{16,24},{20,28},{24,16},{28,20},{1,9},{5... | collective-permute-start | bytes 393224 | tf_op jit(solution)/shard_map/ppermute | solution.py:324
  18.6 6.9 %collective-permute-start.3 = (bf16[256,256]{1,0:T(8,128)(2,1)S(1)}, bf16[256,256]{1,0:T(8,128)(2,1)S(1)}, u32[]{:S(2)}, u32[]{:S(2)}) collective-permute-start(bf16[256,256]{1,0:T(8,128)(2,1)S(1)} %collective-permute-done.1.refs_1_), channel_id=1, source_target_pairs={{0,4},{4,0},{8,12},{12,8},{16,20},{20,16},{24,28},{28,24},{1,5},{5... | collective-permute-start | bytes 393224 | tf_op jit(solution)/shard_map/ppermute | solution.py:324
  28.6 1.9 %collective-permute-start.9 = (bf16[64,2048]{1,0:T(8,128)(2,1)S(1)}, bf16[64,2048]{1,0:T(8,128)(2,1)S(1)}, u32[]{:S(2)}, u32[]{:S(2)}) collective-permute-start(bf16[64,2048]{1,0:T(8,128)(2,1)S(1)} %get-tuple-element.36), channel_id=1, source_target_pairs={{0,1},{1,0},{2,3},{3,2},{4,5},{5,4},{6,7},{7,6},{8,9},{9,8},{10,11... | collective-permute-start | bytes 786440 | tf_op jit(solution)/shard_map/ppermute | solution.py:367
  30.0 2.2 %collective-permute-start.7 = (bf16[64,2048]{1,0:T(8,128)(2,1)S(1)}, bf16[64,2048]{1,0:T(8,128)(2,1)S(1)}, u32[]{:S(2)}, u32[]{:S(2)}) collective-permute-start(bf16[64,2048]{1,0:T(8,128)(2,1)S(1)} %get-tuple-element.34), channel_id=1, source_target_pairs={{0,1},{1,0},{2,3},{3,2},{4,5},{5,4},{6,7},{7,6},{8,9},{9,8},{10,11... | collective-permute-start | bytes 786440 | tf_op jit(solution)/shard_map/ppermute | solution.py:367
  30.6 6.4 %collective-permute-start.10 = (bf16[32,2048]{1,0:T(8,128)(2,1)S(1)}, bf16[32,2048]{1,0:T(8,128)(2,1)S(1)}, u32[]{:S(2)}, u32[]{:S(2)}) collective-permute-start(bf16[32,2048]{1,0:T(8,128)(2,1)S(1)} %add_convert_fusion), channel_id=1, source_target_pairs={{0,2},{1,3},{2,0},{3,1},{4,6},{5,7},{6,4},{7,5},{8,10},{9,11},{10,... | collective-permute-start | bytes 393224 | tf_op jit(solution)/shard_map/ppermute | solution.py:367
  32.2 6.7 %collective-permute-start.8 = (bf16[32,2048]{1,0:T(8,128)(2,1)S(1)}, bf16[32,2048]{1,0:T(8,128)(2,1)S(1)}, u32[]{:S(2)}, u32[]{:S(2)}) collective-permute-start(bf16[32,2048]{1,0:T(8,128)(2,1)S(1)} %add_convert_fusion.1), channel_id=1, source_target_pairs={{0,2},{1,3},{2,0},{3,1},{4,6},{5,7},{6,4},{7,5},{8,10},{9,11},{10,... | collective-permute-start | bytes 393224 | tf_op jit(solution)/shard_map/ppermute | solution.py:367

commit v6 on v5

--- a/solution.py
+++ b/solution.py
@@ -311,7 +311,7 @@
 
 
 SHARES = (3, 4, 1)
-PLAN = ((4, 0, 4), (2, 0, 2), (1, 0, 1), (7, 0, 7), (3, 2, 1), (6, 4, 2), (5, 4, 1))
+PLAN = ((3, 0, 3), (4, 0, 4), (2, 0, 2), (1, 0, 1), (7, 0, 7), (5, 4, 1), (6, 4, 2))
 
 
 def blockwise(n, n_tp, queries, keys, values, doc_blocks, block_order, out_weight):
@@ -345,7 +345,7 @@
         return pltpu.VMEM((min(len(slots), n // 2 - 1),) + kv.shape, bf16)
 
     weights = [weight]
-    for slots, depth in zip(((1, 2, 4), (3, 7, 6)), split[1:]):
+    for slots, depth in zip(((1, 2, 4), (3, 7, 5)), split[1:]):
         first = sum(w.shape[0] for w in weights)
         top, sums, weight = kernel(
             functools.partial(more, slots, first),
@@ -354,7 +354,7 @@
             states + [((depth, out_width), bf16)], [held(slots), dma((depth // 128,))],
             flops=4 * 10**9, aliases={3: 0, 4: 1}, limit=8)
         weights.append(weight)
-    slots = (5,)
+    slots = (6,)
     part, chunk, half = rows // n_tp, 512, out_width // 2
     shares = [((rows // 2, half), bf16), ((rows // 2, half), f32)]
     _, _, att, give0, keep0 = kernel(

time: 39.8 us -> 38.2 us (0.960)
  waiting for transfers between devices: 12.9 us -> 10.4 us
  starting transfers between devices: 12.7 us -> 13.6 us
    ppermute x7, waiting for transfers between devices: 8.09 us -> 5.54 us  [swap(): return lax.ppermute(block, 'cp', [(i, i ^ s) for i in range(n)])]
    ppermute x7, starting transfers between devices: 9.31 us -> 10.3 us  [swap(): return lax.ppermute(block, 'cp', [(i, i ^ s) for i in range(n)])]
  transfers between devices with their start and end apart: 11 -> 11, of which waited for: 4 -> 5; matrix products, arithmetic and copies ran while one was open for 0% -> 0% of each run, Pallas kernels for 27% -> 28%
where the time goes in v6:
time: 38.2 us; the launch traced here: 38.1 us
  Pallas kernels  13.9 us (36%)
  starting transfers between devices  13.6 us (36%)
  waiting for transfers between devices  10.4 us (27%)
    pallas_call x6, Pallas kernels, kernel(): pl.pallas_call(body, out_shape=tuple((pltpu.VMEM(shape, dtype) for shape,...  12.5 us
    ppermute x7, starting transfers between devices, swap(): return lax.ppermute(block, 'cp', [(i, i ^ s) for i in range(n)])  10.3 us
    ppermute x7, waiting for transfers between devices, swap(): return lax.ppermute(block, 'cp', [(i, i ^ s) for i in range(n)])  5.54 us
    ppermute x4, waiting for transfers between devices, across(): return lax.ppermute(x, 'tp', [(i, i ^ hop) for i in range(n_tp)])  4.85 us
    ppermute x4, starting transfers between devices, across(): return lax.ppermute(x, 'tp', [(i, i ^ hop) for i in range(n_tp)])  3.34 us
    pallas_call x2, Pallas kernels, blockwise(): pl.pallas_call(functools.partial(last, i * half), out_shape=(pltpu.HBM((p...  1.41 us
  transfers between devices with their start and end apart: 11, of which 5 were waited for; matrix products, arithmetic and copies ran while one was open for 0% of the time, Pallas kernels for 28%

profile of v6, /device:TPU:0, one launch (start us, length us, event | category | flops | bytes accessed | tf_op | source)
XLA Modules:
  0.0 38.1 jit_solution(16013678866449832643)
XLA Ops:
  0.0 0.9 %shard_map.64.kv_ref = bf16[256,256]{1,0:T(8,128)(2,1)S(1)} custom-call(bf16[128,256]{1,0:T(8,128)(2,1)} %k_hbm.1, bf16[128,256]{1,0:T(8,128)(2,1)} %v_hbm.1), custom_call_target="tpu_custom_call" | custom-call | tf_op jit(solution)/shard_map/pallas_call | solution.py:289
  0.9 6.1 %collective-permute-start.4 = (bf16[256,256]{1,0:T(8,128)(2,1)S(1)}, bf16[256,256]{1,0:T(8,128)(2,1)S(1)}, u32[]{:S(2)}, u32[]{:S(2)}) collective-permute-start(bf16[256,256]{1,0:T(8,128)(2,1)S(1)} %shard_map.64.kv_ref), channel_id=1, source_target_pairs={{0,28},{4,24},{8,20},{12,16},{16,12},{20,8},{24,4},{28,0},{1,29},{... | collective-permute-start | bytes 393224 | tf_op jit(solution)/shard_map/ppermute | solution.py:324
  7.0 0.0 collective-permute-start.3
  7.0 0.6 %collective-permute-start.2 = (bf16[256,256]{1,0:T(8,128)(2,1)S(1)}, bf16[256,256]{1,0:T(8,128)(2,1)S(1)}, u32[]{:S(2)}, u32[]{:S(2)}) collective-permute-start(bf16[256,256]{1,0:T(8,128)(2,1)S(1)} %shard_map.64.kv_ref), channel_id=1, source_target_pairs={{0,16},{4,20},{8,24},{12,28},{16,0},{20,4},{24,8},{28,12},{1,17},{... | collective-permute-start | bytes 393224 | tf_op jit(solution)/shard_map/ppermute | solution.py:324
  7.6 1.4 %collective-permute-start.1 = (bf16[256,256]{1,0:T(8,128)(2,1)S(1)}, bf16[256,256]{1,0:T(8,128)(2,1)S(1)}, u32[]{:S(2)}, u32[]{:S(2)}) collective-permute-start(bf16[256,256]{1,0:T(8,128)(2,1)S(1)} %shard_map.64.kv_ref), channel_id=1, source_target_pairs={{0,8},{4,12},{8,0},{12,4},{16,24},{20,28},{24,16},{28,20},{1,9},{5... | collective-permute-start | bytes 393224 | tf_op jit(solution)/shard_map/ppermute | solution.py:324
  9.0 1.5 %collective-permute-start = (bf16[256,256]{1,0:T(8,128)(2,1)S(1)}, bf16[256,256]{1,0:T(8,128)(2,1)S(1)}, u32[]{:S(2)}, u32[]{:S(2)}) collective-permute-start(bf16[256,256]{1,0:T(8,128)(2,1)S(1)} %shard_map.64.kv_ref), channel_id=1, source_target_pairs={{0,4},{4,0},{8,12},{12,8},{16,20},{20,16},{24,28},{28,24},{1,5},{5... | collective-permute-start | bytes 393224 | tf_op jit(solution)/shard_map/ppermute | solution.py:324
  10.5 3.7 %shard_map.65 = (bf16[2048,128]{1,0:T(8,128)(2,1)S(1)}, s32[8,128]{1,0:T(8,128)S(1)}, f32[2048,128]{1,0:T(8,128)S(1)}, f32[2048,256]{1,0:T(8,128)S(1)}, bf16[768,4096]{1,0:T(8,128)(2,1)S(1)}) custom-call(s32[8]{0:T(128)} %order_hbm.1, s32[4]{0:T(128)} %docs_hbm.1, bf16[128,2048]{1,0:T(8,128)(2,1)} %q_hbm.1, bf16[2048,4096]{1,0:T(8,128)(2,1)} %w_hbm.5, ...), custom_call_target="tpu_custom_call" | custom-call | flops 4000000000 | tf_op jit(solution)/shard_map/pallas_call | solution.py:289
  14.1 4.0 %collective-permute-done.2.refs_2_ = bf16[256,256]{1,0:T(8,128)(2,1)S(1)} collective-permute-done((bf16[256,256]{1,0:T(8,128)(2,1)S(1)}, bf16[256,256]{1,0:T(8,128)(2,1)S(1)}, u32[]{:S(2)}, u32[]{:S(2)}) %collective-permute-start.2) | collective-permute-done | bytes 131104 | tf_op jit(solution)/shard_map/ppermute | solution.py:324
  18.1 0.0 collective-permute-start.6
  18.1 0.8 %collective-permute-done.1.refs_1_ = bf16[256,256]{1,0:T(8,128)(2,1)S(1)} collective-permute-done((bf16[256,256]{1,0:T(8,128)(2,1)S(1)}, bf16[256,256]{1,0:T(8,128)(2,1)S(1)}, u32[]{:S(2)}, u32[]{:S(2)}) %collective-permute-start.1) | collective-permute-done | bytes 131104 | tf_op jit(solution)/shard_map/ppermute | solution.py:324
  18.9 0.7 %collective-permute-start.5 = (bf16[256,256]{1,0:T(8,128)(2,1)S(1)}, bf16[256,256]{1,0:T(8,128)(2,1)S(1)}, u32[]{:S(2)}, u32[]{:S(2)}) collective-permute-start(bf16[256,256]{1,0:T(8,128)(2,1)S(1)} %collective-permute-done.2.refs_2_), channel_id=1, source_target_pairs={{0,4},{4,0},{8,12},{12,8},{16,20},{20,16},{24,28},{28,24},{1,5},{5... | collective-permute-start | bytes 393224 | tf_op jit(solution)/shard_map/ppermute | solution.py:324
  19.7 0.0 collective-permute-done.refs_0_
  19.7 3.5 %shard_map.66 = (f32[2048,128]{1,0:T(8,128)S(1)}, f32[2048,256]{1,0:T(8,128)S(1)}, bf16[1024,4096]{1,0:T(8,128)(2,1)S(1)}) custom-call(s32[8,128]{1,0:T(8,128)S(1)} %get-tuple-element.21.seen_ref, bf16[2048,4096]{1,0:T(8,128)(2,1)} %w_hbm.5, bf16[2048,128]{1,0:T(8,128)(2,1)S(1)} %get-tuple-element.22.qr_ref, ...), custom_call_target="tpu_custom_call", output_to_operand_aliasing={{0}: (3, {}), {1}: (4, {})} | custom-call | flops 4000000000 | tf_op jit(solution)/shard_map/pallas_call | solution.py:289
  23.2 0.0 collective-permute-done.4.refs_1_
  23.2 0.0 collective-permute-done.3.refs_0_
  23.2 0.7 %collective-permute-done.5.refs_2_ = bf16[256,256]{1,0:T(8,128)(2,1)S(1)} collective-permute-done((bf16[256,256]{1,0:T(8,128)(2,1)S(1)}, bf16[256,256]{1,0:T(8,128)(2,1)S(1)}, u32[]{:S(2)}, u32[]{:S(2)}) %collective-permute-start.5) | collective-permute-done | bytes 131104 | tf_op jit(solution)/shard_map/ppermute | solution.py:324
  23.9 1.6 %shard_map.67 = (f32[2048,128]{1,0:T(8,128)S(1)}, f32[2048,256]{1,0:T(8,128)S(1)}, bf16[256,4096]{1,0:T(8,128)(2,1)S(1)}) custom-call(s32[8,128]{1,0:T(8,128)S(1)} %get-tuple-element.21.seen_ref, bf16[2048,4096]{1,0:T(8,128)(2,1)} %w_hbm.5, bf16[2048,128]{1,0:T(8,128)(2,1)S(1)} %get-tuple-element.22.qr_ref, ...), custom_call_target="tpu_custom_call", output_to_operand_aliasing={{0}: (3, {}), {1}: (4, {})} | custom-call | flops 4000000000 | tf_op jit(solution)/shard_map/pallas_call | solution.py:289
  25.6 0.0 collective-permute-done.6.refs_0_
  25.6 1.5 %shard_map.68 = (f32[2048,128]{1,0:T(8,128)S(1)}, f32[2048,256]{1,0:T(8,128)S(1)}, bf16[128,2048]{1,0:T(8,128)(2,1)S(1)}, bf16[64,2048]{1,0:T(8,128)(2,1)S(1)}, f32[64,2048]{1,0:T(8,128)S(1)}) custom-call(s32[8,128]{1,0:T(8,128)S(1)} %get-tuple-element.21.seen_ref, ...), custom_call_target="tpu_custom_call", output_to_operand_aliasing={{0}: (2, {}), {1}: (3, {})} | custom-call | flops 1073741824 | tf_op jit(solution)/shard_map/pallas_call | solution.py:289
  27.1 0.1 collective-permute-start.9
  27.2 1.3 %shard_map.69 = (bf16[64,2048]{1,0:T(8,128)(2,1)S(1)}, f32[64,2048]{1,0:T(8,128)S(1)}) custom-call(bf16[128,2048]{1,0:T(8,128)(2,1)S(1)} %get-tuple-element.32.att_ref, bf16[768,4096]{1,0:T(8,128)(2,1)S(1)} %get-tuple-element.29.refs_1_.refs_0_, bf16[1024,4096]{1,0:T(8,128)(2,1)S(1)} %get-tuple-element.30.refs_2_.refs_1_, ...), custom_call_target="tpu_custom_call" | custom-call | flops 1073741824 | tf_op jit(solution)/shard_map/pallas_call | solution.py:289
  28.5 0.6 %collective-permute-start.7 = (bf16[64,2048]{1,0:T(8,128)(2,1)S(1)}, bf16[64,2048]{1,0:T(8,128)(2,1)S(1)}, u32[]{:S(2)}, u32[]{:S(2)}) collective-permute-start(bf16[64,2048]{1,0:T(8,128)(2,1)S(1)} %get-tuple-element.34), channel_id=1, source_target_pairs={{0,1},{1,0},{2,3},{3,2},{4,5},{5,4},{6,7},{7,6},{8,9},{9,8},{10,11... | collective-permute-start | bytes 786440 | tf_op jit(solution)/shard_map/ppermute | solution.py:367
  29.0 0.0 collective-permute-done.9.other_ref
  29.1 1.6 %collective-permute-start.10 = (bf16[32,2048]{1,0:T(8,128)(2,1)S(1)}, bf16[32,2048]{1,0:T(8,128)(2,1)S(1)}, u32[]{:S(2)}, u32[]{:S(2)}) collective-permute-start(bf16[32,2048]{1,0:T(8,128)(2,1)S(1)} %add_convert_fusion), channel_id=1, source_target_pairs={{0,2},{1,3},{2,0},{3,1},{4,6},{5,7},{6,4},{7,5},{8,10},{9,11},{10,... | collective-permute-start | bytes 393224 | tf_op jit(solution)/shard_map/ppermute | solution.py:367
  30.7 0.0 collective-permute-done.7.other_ref
  30.7 1.1 %collective-permute-start.8 = (bf16[32,2048]{1,0:T(8,128)(2,1)S(1)}, bf16[32,2048]{1,0:T(8,128)(2,1)S(1)}, u32[]{:S(2)}, u32[]{:S(2)}) collective-permute-start(bf16[32,2048]{1,0:T(8,128)(2,1)S(1)} %add_convert_fusion.1), channel_id=1, source_target_pairs={{0,2},{1,3},{2,0},{3,1},{4,6},{5,7},{6,4},{7,5},{8,10},{9,11},{10,... | collective-permute-start | bytes 393224 | tf_op jit(solution)/shard_map/ppermute | solution.py:367
  31.8 3.7 %collective-permute-done.10.crossed_ref = bf16[32,2048]{1,0:T(8,128)(2,1)S(1)} collective-permute-done((bf16[32,2048]{1,0:T(8,128)(2,1)S(1)}, bf16[32,2048]{1,0:T(8,128)(2,1)S(1)}, u32[]{:S(2)}, u32[]{:S(2)}) %collective-permute-start.10) | collective-permute-done | bytes 131104 | tf_op jit(solution)/shard_map/ppermute | solution.py:367
  35.5 0.7 %shard_map.70.refs_0_ = bf16[32,4096]{1,0:T(8,128)(2,1)} custom-call(f32[64,2048]{1,0:T(8,128)S(1)} %get-tuple-element.35.keep_ref, bf16[64,2048]{1,0:T(8,128)(2,1)S(1)} %collective-permute-done.9.other_ref, bf16[32,2048]{1,0:T(8,128)(2,1)S(1)} %collective-permute-done.10.crossed_ref), custom_call_target="tpu_custom_call" | custom-call | tf_op jit(solution)/shard_map/pallas_call | solution.py:381
  36.2 1.2 %collective-permute-done.8.crossed_ref = bf16[32,2048]{1,0:T(8,128)(2,1)S(1)} collective-permute-done((bf16[32,2048]{1,0:T(8,128)(2,1)S(1)}, bf16[32,2048]{1,0:T(8,128)(2,1)S(1)}, u32[]{:S(2)}, u32[]{:S(2)}) %collective-permute-start.8) | collective-permute-done | bytes 131104 | tf_op jit(solution)/shard_map/ppermute | solution.py:367
  37.4 0.7 %shard_map.71 = bf16[32,4096]{1,0:T(8,128)(2,1)} custom-call(f32[64,2048]{1,0:T(8,128)S(1)} %get-tuple-element.33.keep_ref, bf16[64,2048]{1,0:T(8,128)(2,1)S(1)} %collective-permute-done.7.other_ref, bf16[32,2048]{1,0:T(8,128)(2,1)S(1)} %collective-permute-done.8.crossed_ref, bf16[32,4096]{1,0:T(8,128)(2,1)} %shard_map.70.refs_0_), custom_call_target="tpu_custom_call", output_to_operand_aliasing={{}: (3, {})} | custom-call | tf_op jit(solution)/shard_map/pallas_call | solution.py:381
  (2 shorter events, 0.1 us)
Async XLA Ops:
  0.9 22.3 %collective-permute-start.4 = (bf16[256,256]{1,0:T(8,128)(2,1)S(1)}, bf16[256,256]{1,0:T(8,128)(2,1)S(1)}, u32[]{:S(2)}, u32[]{:S(2)}) collective-permute-start(bf16[256,256]{1,0:T(8,128)(2,1)S(1)} %shard_map.64.kv_ref), channel_id=1, source_target_pairs={{0,28},{4,24},{8,20},{12,16},{16,12},{20,8},{24,4},{28,0},{1,29},{... | collective-permute-start | bytes 393224 | tf_op jit(solution)/shard_map/ppermute | solution.py:324
  7.0 16.2 %collective-permute-start.3 = (bf16[256,256]{1,0:T(8,128)(2,1)S(1)}, bf16[256,256]{1,0:T(8,128)(2,1)S(1)}, u32[]{:S(2)}, u32[]{:S(2)}) collective-permute-start(bf16[256,256]{1,0:T(8,128)(2,1)S(1)} %shard_map.64.kv_ref), channel_id=1, source_target_pairs={{0,12},{4,8},{8,4},{12,0},{16,28},{20,24},{24,20},{28,16},{1,13},{... | collective-permute-start | bytes 393224 | tf_op jit(solution)/shard_map/ppermute | solution.py:324
  7.0 11.2 %collective-permute-start.2 = (bf16[256,256]{1,0:T(8,128)(2,1)S(1)}, bf16[256,256]{1,0:T(8,128)(2,1)S(1)}, u32[]{:S(2)}, u32[]{:S(2)}) collective-permute-start(bf16[256,256]{1,0:T(8,128)(2,1)S(1)} %shard_map.64.kv_ref), channel_id=1, source_target_pairs={{0,16},{4,20},{8,24},{12,28},{16,0},{20,4},{24,8},{28,12},{1,17},{... | collective-permute-start | bytes 393224 | tf_op jit(solution)/shard_map/ppermute | solution.py:324
  7.6 11.3 %collective-permute-start.1 = (bf16[256,256]{1,0:T(8,128)(2,1)S(1)}, bf16[256,256]{1,0:T(8,128)(2,1)S(1)}, u32[]{:S(2)}, u32[]{:S(2)}) collective-permute-start(bf16[256,256]{1,0:T(8,128)(2,1)S(1)} %shard_map.64.kv_ref), channel_id=1, source_target_pairs={{0,8},{4,12},{8,0},{12,4},{16,24},{20,28},{24,16},{28,20},{1,9},{5... | collective-permute-start | bytes 393224 | tf_op jit(solution)/shard_map/ppermute | solution.py:324
  9.0 10.7 %collective-permute-start = (bf16[256,256]{1,0:T(8,128)(2,1)S(1)}, bf16[256,256]{1,0:T(8,128)(2,1)S(1)}, u32[]{:S(2)}, u32[]{:S(2)}) collective-permute-start(bf16[256,256]{1,0:T(8,128)(2,1)S(1)} %shard_map.64.kv_ref), channel_id=1, source_target_pairs={{0,4},{4,0},{8,12},{12,8},{16,20},{20,16},{24,28},{28,24},{1,5},{5... | collective-permute-start | bytes 393224 | tf_op jit(solution)/shard_map/ppermute | solution.py:324
  18.1 7.4 %collective-permute-start.6 = (bf16[256,256]{1,0:T(8,128)(2,1)S(1)}, bf16[256,256]{1,0:T(8,128)(2,1)S(1)}, u32[]{:S(2)}, u32[]{:S(2)}) collective-permute-start(bf16[256,256]{1,0:T(8,128)(2,1)S(1)} %collective-permute-done.2.refs_2_), channel_id=1, source_target_pairs={{0,8},{4,12},{8,0},{12,4},{16,24},{20,28},{24,16},{28,20},{1,9},{5... | collective-permute-start | bytes 393224 | tf_op jit(solution)/shard_map/ppermute | solution.py:324
  18.9 5.0 %collective-permute-start.5 = (bf16[256,256]{1,0:T(8,128)(2,1)S(1)}, bf16[256,256]{1,0:T(8,128)(2,1)S(1)}, u32[]{:S(2)}, u32[]{:S(2)}) collective-permute-start(bf16[256,256]{1,0:T(8,128)(2,1)S(1)} %collective-permute-done.2.refs_2_), channel_id=1, source_target_pairs={{0,4},{4,0},{8,12},{12,8},{16,20},{20,16},{24,28},{28,24},{1,5},{5... | collective-permute-start | bytes 393224 | tf_op jit(solution)/shard_map/ppermute | solution.py:324
  27.1 1.9 %collective-permute-start.9 = (bf16[64,2048]{1,0:T(8,128)(2,1)S(1)}, bf16[64,2048]{1,0:T(8,128)(2,1)S(1)}, u32[]{:S(2)}, u32[]{:S(2)}) collective-permute-start(bf16[64,2048]{1,0:T(8,128)(2,1)S(1)} %get-tuple-element.36), channel_id=1, source_target_pairs={{0,1},{1,0},{2,3},{3,2},{4,5},{5,4},{6,7},{7,6},{8,9},{9,8},{10,11... | collective-permute-start | bytes 786440 | tf_op jit(solution)/shard_map/ppermute | solution.py:367
  28.5 2.2 %collective-permute-start.7 = (bf16[64,2048]{1,0:T(8,128)(2,1)S(1)}, bf16[64,2048]{1,0:T(8,128)(2,1)S(1)}, u32[]{:S(2)}, u32[]{:S(2)}) collective-permute-start(bf16[64,2048]{1,0:T(8,128)(2,1)S(1)} %get-tuple-element.34), channel_id=1, source_target_pairs={{0,1},{1,0},{2,3},{3,2},{4,5},{5,4},{6,7},{7,6},{8,9},{9,8},{10,11... | collective-permute-start | bytes 786440 | tf_op jit(solution)/shard_map/ppermute | solution.py:367
  29.1 6.4 %collective-permute-start.10 = (bf16[32,2048]{1,0:T(8,128)(2,1)S(1)}, bf16[32,2048]{1,0:T(8,128)(2,1)S(1)}, u32[]{:S(2)}, u32[]{:S(2)}) collective-permute-start(bf16[32,2048]{1,0:T(8,128)(2,1)S(1)} %add_convert_fusion), channel_id=1, source_target_pairs={{0,2},{1,3},{2,0},{3,1},{4,6},{5,7},{6,4},{7,5},{8,10},{9,11},{10,... | collective-permute-start | bytes 393224 | tf_op jit(solution)/shard_map/ppermute | solution.py:367
  30.7 6.7 %collective-permute-start.8 = (bf16[32,2048]{1,0:T(8,128)(2,1)S(1)}, bf16[32,2048]{1,0:T(8,128)(2,1)S(1)}, u32[]{:S(2)}, u32[]{:S(2)}) collective-permute-start(bf16[32,2048]{1,0:T(8,128)(2,1)S(1)} %add_convert_fusion.1), channel_id=1, source_target_pairs={{0,2},{1,3},{2,0},{3,1},{4,6},{5,7},{6,4},{7,5},{8,10},{9,11},{10,... | collective-permute-start | bytes 393224 | tf_op jit(solution)/shard_map/ppermute | solution.py:367
